TPU v7x, 32 devices: a whole 2x2x4 slice. The times are simulated.
32 devices in a mesh: depth: 4 (over z), col: 2 (over y), row: 4 (over x, core).
Axes of the slice: x: 2, y: 2, z: 4, core: 2. Of those that a mesh axis runs over, the one named last changes fastest.
Arguments:
- reach_in: bfloat16 [2048, 2048], P(('row', 'depth'), 'col')
Outputs:
- output: bfloat16 [2048, 2048], P(('row', 'depth'), 'col')
All inputs are finite; a program needn't handle non-finite values.
Results may differ from a plain program's by a relative error of at most 0.001.
Values are sent between devices in bfloat16 or wider.
A program may use at most 1 GiB of HBM per device.

v0:
```python
import jax
import jax.numpy as jnp
from jax import lax
from jax.sharding import PartitionSpec as P

SQUARINGS = 4


def solution(mesh):
    depth_size = mesh.shape['depth']
    col_size = mesh.shape['col']
    row_size = mesh.shape['row']
    col_ratio = row_size // col_size
    per_layer = row_size // depth_size
    n_used = min(col_ratio, per_layer)
    all_axes = ('depth', 'col', 'row')

    def linear(layer_id, col_id, row_id):
        return (layer_id * col_size + col_id) * row_size + row_id

    def a_perm(piece_id):
        perm_pairs = []
        for layer_id in range(depth_size):
            for col_id in range(col_size):
                for row_id in range(row_size):
                    offset = (row_id + layer_id * per_layer + piece_id) // col_ratio
                    perm_pairs.append((linear(layer_id, col_id, row_id), linear(layer_id, (col_id - offset) % col_size, row_id)))
        return perm_pairs

    def b_perm():
        perm_pairs = []
        for layer_id in range(depth_size):
            for col_id in range(col_size):
                for k_id in range(row_size):
                    dest_row = (k_id - col_id * col_ratio - layer_id * per_layer) % row_size
                    perm_pairs.append((linear(layer_id, col_id, k_id), linear(layer_id, col_id, dest_row)))
        return perm_pairs

    a_perms = [a_perm(piece_id) for piece_id in range(n_used)]
    b_skew = b_perm()
    col_shift = [(col_id, (col_id - 1) % col_size) for col_id in range(col_size)]
    row_shift = [(row_id, (row_id - 1) % row_size) for row_id in range(row_size)]

    def local_squarings(row_slab):
        row_idx = lax.axis_index('row')
        layer_idx = lax.axis_index('depth')
        for _ in range(SQUARINGS):
            full_block = lax.all_gather(row_slab, 'depth', axis=0, tiled=True)
            k_width = full_block.shape[0]
            window = []
            for piece_id in range(n_used):
                if col_ratio == 1:
                    a_piece = full_block
                else:
                    sub_idx = (row_idx + layer_idx * per_layer + piece_id) % col_ratio
                    a_piece = lax.dynamic_slice_in_dim(full_block, sub_idx * k_width, k_width, axis=1)
                window.append(lax.ppermute(a_piece, all_axes, a_perms[piece_id]))
            b_block = lax.ppermute(full_block, all_axes, b_skew)
            partial_sum = None
            for step_id in range(per_layer):
                slot_id = step_id % col_ratio
                product = jnp.dot(window[slot_id], b_block, preferred_element_type=jnp.float32)
                partial_sum = product if partial_sum is None else partial_sum + product
                if step_id + col_ratio < per_layer:
                    window[slot_id] = lax.ppermute(window[slot_id], 'col', col_shift)
                if step_id + 1 < per_layer:
                    b_block = lax.ppermute(b_block, 'row', row_shift)
            reduced = lax.psum_scatter(partial_sum, 'depth', scatter_dimension=0, tiled=True)
            row_slab = jnp.minimum(reduced + row_slab.astype(jnp.float32), 1.0).astype(jnp.bfloat16)
        return row_slab

    layout = P(('row', 'depth'), 'col')
    return jax.shard_map(local_squarings, mesh=mesh, in_specs=(layout,), out_specs=layout, check_vma=False)
```

profile of v0, /device:TPU:0, one launch (start us, length us, event | category | flops | bytes accessed | tf_op | source)
XLA Modules:
  0.0 417.9 jit_solution(11105491613503248848)
XLA Ops:
  6.5 0.7 all-gather.5.cloned.1.call-update
  7.3 32.3 %all-gather.5.cloned.1.call-done = bf16[512,1024]{1,0:T(8,128)(2,1)} async-done(((bf16[128,1024]{1,0:T(8,128)(2,1)}), bf16[512,1024]{1,0:T(8,128)(2,1)}) %all-gather.5.cloned.1.call-update) | async-done | bytes 1048592 | tf_op jit(solution)/shard_map/all_gather | solution.py:48
  39.6 1.9 collective-permute-start.1
  41.5 1.1 constant_dynamic-slice_fusion.3
  42.6 0.8 collective-permute-start
  43.4 2.1 fusion
  45.5 0.0 all-gather.7.cloned.1.call-start
  45.5 64.8 %reduce-scatter.5.cloned.1.call-done = f32[128,1024]{1,0:T(8,128)} async-done(((f32[512,1024]{1,0:T(8,128)}), f32[128,1024]{1,0:T(8,128)}) %reduce-scatter.5.cloned.1.call-update) | async-done | bytes 524304 | tf_op jit(solution)/shard_map/reduce_scatter | solution.py:68
  110.4 1.8 minimum_convert_fusion.3
  112.3 27.0 %all-gather.7.cloned.1.call-done = bf16[512,1024]{1,0:T(8,128)(2,1)} async-done(((bf16[128,1024]{1,0:T(8,128)(2,1)}), bf16[512,1024]{1,0:T(8,128)(2,1)}) %all-gather.7.cloned.1.call-update) | async-done | bytes 1048592 | tf_op jit(solution)/shard_map/all_gather | solution.py:48
  139.2 1.9 collective-permute-start.3
  141.1 1.1 constant_dynamic-slice_fusion.2
  142.2 0.8 collective-permute-start.2
  143.0 2.1 fusion.1
  145.1 0.0 all-gather.9.cloned.1.call-start
  145.2 64.8 %reduce-scatter.7.cloned.1.call-done = f32[128,1024]{1,0:T(8,128)} async-done(((f32[512,1024]{1,0:T(8,128)}), f32[128,1024]{1,0:T(8,128)}) %reduce-scatter.7.cloned.1.call-update) | async-done | bytes 524304 | tf_op jit(solution)/shard_map/reduce_scatter | solution.py:68
  210.0 1.8 minimum_convert_fusion.2
  211.9 27.0 %all-gather.9.cloned.1.call-done = bf16[512,1024]{1,0:T(8,128)(2,1)} async-done(((bf16[128,1024]{1,0:T(8,128)(2,1)}), bf16[512,1024]{1,0:T(8,128)(2,1)}) %all-gather.9.cloned.1.call-update) | async-done | bytes 1048592 | tf_op jit(solution)/shard_map/all_gather | solution.py:48
  238.8 1.9 collective-permute-start.5
  240.7 1.1 constant_dynamic-slice_fusion.1
  241.8 0.8 collective-permute-start.4
  242.6 2.1 fusion.2
  244.7 0.0 all-gather.11.cloned.1.call-start
  244.8 64.8 %reduce-scatter.9.cloned.1.call-done = f32[128,1024]{1,0:T(8,128)} async-done(((f32[512,1024]{1,0:T(8,128)}), f32[128,1024]{1,0:T(8,128)}) %reduce-scatter.9.cloned.1.call-update) | async-done | bytes 524304 | tf_op jit(solution)/shard_map/reduce_scatter | solution.py:68
  309.6 1.8 minimum_convert_fusion.1
  311.5 27.0 %all-gather.11.cloned.1.call-done = bf16[512,1024]{1,0:T(8,128)(2,1)} async-done(((bf16[128,1024]{1,0:T(8,128)(2,1)}), bf16[512,1024]{1,0:T(8,128)(2,1)}) %all-gather.11.cloned.1.call-update) | async-done | bytes 1048592 | tf_op jit(solution)/shard_map/all_gather | solution.py:48
  338.4 1.9 collective-permute-start.7
  340.3 1.1 constant_dynamic-slice_fusion
  341.4 0.8 collective-permute-start.6
  342.3 2.1 fusion.3
  344.3 64.9 %reduce-scatter.11.cloned.1.call-done = f32[128,1024]{1,0:T(8,128)} async-done(((f32[512,1024]{1,0:T(8,128)}), f32[128,1024]{1,0:T(8,128)}) %reduce-scatter.11.cloned.1.call-update) | async-done | bytes 524304 | tf_op jit(solution)/shard_map/reduce_scatter | solution.py:68
  409.2 1.8 minimum_convert_fusion
  (28 shorter events, 0.3 us)
Async XLA Ops:
  6.5 33.1 %all-gather.5.cloned.1.call-start = ((), (), s32[]{:S(2)}) async-start(), calls=%async_computation.4 | async-start | bytes 1310720 | tf_op jit(solution)/shard_map/all_gather | solution.py:48
  7.3 103.1 %reduce-scatter.5.cloned.1.call-start = ((), (), s32[]{:S(2)}) async-start(), calls=%async_computation.5 | async-start | bytes 2621440 | tf_op jit(solution)/shard_map/reduce_scatter | solution.py:68
  39.6 3.8 collective-permute-start.1
  42.5 67.8 %copy-start.3 = (bf16[128,1024]{1,0:T(8,128)(2,1)S(1)}, bf16[128,1024]{1,0:T(8,128)(2,1)}, u32[]{:S(2)}) copy-start(bf16[128,1024]{1,0:T(8,128)(2,1)} %param.1) | copy-start | bytes 786436
  42.6 0.8 collective-permute-start
  45.5 93.7 %all-gather.7.cloned.1.call-start = ((), (), s32[]{:S(2)}) async-start(), calls=%async_computation.6 | async-start | bytes 1310720 | tf_op jit(solution)/shard_map/all_gather | solution.py:48
  112.2 97.8 %reduce-scatter.7.cloned.1.call-start = ((), (), s32[]{:S(2)}) async-start(), calls=%async_computation.7 | async-start | bytes 2621440 | tf_op jit(solution)/shard_map/reduce_scatter | solution.py:68
  139.2 3.8 collective-permute-start.3
  142.2 67.8 %copy-start.1 = (bf16[128,1024]{1,0:T(8,128)(2,1)S(1)}, bf16[128,1024]{1,0:T(8,128)(2,1)}, u32[]{:S(2)}) copy-start(bf16[128,1024]{1,0:T(8,128)(2,1)} %minimum_convert_fusion.3) | copy-start | bytes 786436
  142.2 0.8 collective-permute-start.2
  145.1 93.7 %all-gather.9.cloned.1.call-start = ((), (), s32[]{:S(2)}) async-start(), calls=%async_computation.8 | async-start | bytes 1310720 | tf_op jit(solution)/shard_map/all_gather | solution.py:48
  211.8 97.8 %reduce-scatter.9.cloned.1.call-start = ((), (), s32[]{:S(2)}) async-start(), calls=%async_computation.9 | async-start | bytes 2621440 | tf_op jit(solution)/shard_map/reduce_scatter | solution.py:68
  238.8 3.8 collective-permute-start.5
  241.8 67.8 %copy-start = (bf16[128,1024]{1,0:T(8,128)(2,1)S(1)}, bf16[128,1024]{1,0:T(8,128)(2,1)}, u32[]{:S(2)}) copy-start(bf16[128,1024]{1,0:T(8,128)(2,1)} %minimum_convert_fusion.2) | copy-start | bytes 786436
  241.8 0.8 collective-permute-start.4
  244.7 93.7 %all-gather.11.cloned.1.call-start = ((), (), s32[]{:S(2)}) async-start(), calls=%async_computation.10 | async-start | bytes 1310720 | tf_op jit(solution)/shard_map/all_gather | solution.py:48
  311.4 97.8 %reduce-scatter.11.cloned.1.call-start = ((), (), s32[]{:S(2)}) async-start(), calls=%async_computation.11 | async-start | bytes 2621440 | tf_op jit(solution)/shard_map/reduce_scatter | solution.py:68
  338.4 3.8 collective-permute-start.7
  341.4 67.8 %copy-start.2 = (bf16[128,1024]{1,0:T(8,128)(2,1)S(1)}, bf16[128,1024]{1,0:T(8,128)(2,1)}, u32[]{:S(2)}) copy-start(bf16[128,1024]{1,0:T(8,128)(2,1)} %minimum_convert_fusion.1) | copy-start | bytes 786436
  341.4 0.8 collective-permute-start.6
Sparse Core Ops, SparseCore 0:
  8.9 30.6 all-gather.4
  45.6 64.6 reduce-scatter.4
  112.3 26.8 all-gather.6
  145.2 64.7 reduce-scatter.6
  211.9 26.8 all-gather.8
  244.8 64.7 reduce-scatter.8
  311.6 26.8 all-gather.10
  344.5 64.6 reduce-scatter.10
where the time goes:
time: 419 us; the launch traced here: 418 us
  waiting for transfers between devices  373 us (89%)
  between operations  13.6 us (3%)
  starting transfers between devices  11.1 us (3%)
  matrix products  8.21 us (2%)
  other arithmetic  7.25 us (2%)
  local copies, waits for them, and re-layouts  4.33 us (1%)
    reduce_scatter x4, waiting for transfers between devices, local_squarings(): lax.psum_scatter(partial_sum, 'depth', scatter_dimension=0, tiled=True)  259 us
    all_gather x4, waiting for transfers between devices, local_squarings(): full_block = lax.all_gather(row_slab, 'depth', axis=0, tiled=True)  113 us
  transfers between devices with their start and end apart: 16, of which 8 were waited for; matrix products, arithmetic and copies ran while one was open for 1% of the time, Pallas kernels for 0%

commit v1 on v0

v1 whole, which is shorter than its diff:
```python
import jax
import jax.numpy as jnp
from jax import lax
from jax.experimental import pallas as pl
from jax.experimental.pallas import tpu as pltpu
from jax.sharding import PartitionSpec as P

N = 2048
SLAB = 128
HALF = 1024
STEPS = 15
MESH = pl.DeviceIdType.MESH

PIECES = (('zxy', 0, 48), ('zyx', 48, 48), ('xyz', 96, 16), ('yxz', 112, 16))
END_ORDER = (
    1, 4, 8, 17, 20, 24, 33, 36, 40, 49, 52, 56, 2, 9, 5, 12, 18, 25, 28, 34, 37, 41, 21, 44, 60, 57, 50, 53, 10, 6,
    13, 3, 26, 19, 22, 29, 35, 38, 42, 58, 14, 11, 51, 54, 7, 27, 39, 43, 55, 59, 23, 30, 45, 61, 47, 15, 63, 46, 62, 31,
)
MID_ORDER = (
    1, 2, 4, 8, 17, 18, 20, 24, 33, 34, 36, 40, 49, 50, 52, 56, 3, 37, 41, 9, 10, 53, 57, 5, 6, 19, 12, 35, 38, 42,
    58, 51, 54, 25, 26, 28, 21, 22, 39, 43, 45, 61, 55, 59, 44, 60, 7, 11, 47, 63, 46, 27, 62, 13, 14, 29, 30, 23, 15, 31,
)


def forwards(order, dx, dy, k, end):
    far = {'x': dx == 1, 'y': dy == 1, 'z': k != 0}
    last = max([i for i, axis in enumerate(order) if far[axis]], default=-1)
    hops = []
    for i, axis in enumerate(order):
        if axis == 'z' and i > last:
            hops += ['in'] if end else ['in', 'out']
        elif axis == 'z' and i == last and not end:
            hops += ['in'] if k == 1 else ['out']
        elif i > last:
            hops.append(axis)
    return hops


def kernel(in_ref, out_ref, reach, rows, in_sem, send_sem, recv_sem, pass_sem, got_sem):
    z, y, row = lax.axis_index('depth'), lax.axis_index('col'), lax.axis_index('row')
    x, core = row // 2, row % 2
    upper = z >= 2
    z_in = jnp.where(upper, z - 1, z + 1)
    z_out = jnp.where(upper, z + 1, z - 1)
    end = (z == 0) | (z == 3)
    x_row = (1 - x) * 2 + core
    mate_row = x * 2 + 1 - core
    peers = {
        'x': {'depth': z, 'col': y, 'row': x_row},
        'y': {'depth': z, 'col': 1 - y, 'row': row},
        'in': {'depth': z_in, 'col': y, 'row': row},
        'out': {'depth': z_out, 'col': y, 'row': row},
    }
    mate = {'depth': z, 'col': y, 'row': mate_row}

    def slab_at(sx, sy, sz, score):
        return sy, (sx * 2 + score) * 4 + sz

    own_half, own_block = slab_at(x, y, z, core)
    own_row = pl.multiple_of(own_block * SLAB, SLAB)
    load = pltpu.make_async_copy(in_ref, reach.at[own_half, pl.ds(own_row, SLAB), :], in_sem)
    load.start()

    barrier = pltpu.get_barrier_semaphore()
    for name in ('x', 'y', 'in'):
        pl.semaphore_signal(barrier, inc=1, device_id=peers[name], device_id_type=MESH)
    pl.semaphore_signal(barrier, inc=1, device_id=mate, device_id_type=MESH)

    @pl.when(jnp.logical_not(end))
    def _():
        pl.semaphore_signal(barrier, inc=1, device_id=peers['out'], device_id_type=MESH)
        pl.semaphore_wait(barrier, 5)

    @pl.when(end)
    def _():
        pl.semaphore_wait(barrier, 4)

    load.wait()

    def piece_ref(p, sx, sy, sz, score):
        half, block = slab_at(sx, sy, sz, score)
        start = pl.multiple_of(block * SLAB + PIECES[p][1], 16)
        return reach.at[half, pl.ds(start, PIECES[p][2]), :]

    def copy(p, sx, sy, sz, score, peer, send, recv):
        ref = piece_ref(p, sx, sy, sz, score)
        return pltpu.make_async_remote_copy(
            src_ref=ref, dst_ref=ref, send_sem=send, recv_sem=recv, device_id=peer, device_id_type=MESH
        )

    def gather(end_case):
        places = (0, 1, 2, 3) if end_case else (1, 0, 2, 3)

        def source(dx, dy, k):
            sx = (1 - x) if dx else x
            sy = (1 - y) if dy else y
            if k == 0:
                return sx, sy, z
            place = places[k]
            return sx, sy, jnp.where(upper, 3 - place, place)

        sent = [0] * len(PIECES)

        def push(p, dx, dy, k):
            sx, sy, sz = source(dx, dy, k)
            for hop in forwards(PIECES[p][0], dx, dy, k, end_case):
                sent[p] += 1
                copy(p, sx, sy, sz, core, peers[hop], send_sem.at[p], recv_sem.at[p, sx, sy, sz]).start()
            copy(p, sx, sy, sz, core, mate, pass_sem.at[p], got_sem.at[p, sx, sy, sz]).start()

        for p in range(len(PIECES)):
            push(p, 0, 0, 0)
        for code in END_ORDER if end_case else MID_ORDER:
            p, dx, dy, k = code // 16, code // 8 % 2, code // 4 % 2, code % 4
            sx, sy, sz = source(dx, dy, k)
            copy(p, sx, sy, sz, core, mate, send_sem.at[p], recv_sem.at[p, sx, sy, sz]).wait_recv()
            push(p, dx, dy, k)
        for p in range(len(PIECES)):
            drain = copy(p, x, y, z, core, mate, send_sem.at[p], got_sem.at[p, x, y, z])
            for _ in range(sent[p]):
                drain.wait_send()
            drain = copy(p, x, y, z, core, mate, pass_sem.at[p], got_sem.at[p, x, y, z])
            for _ in range(16):
                drain.wait_send()

    @pl.when(end)
    def _():
        gather(True)

    @pl.when(jnp.logical_not(end))
    def _():
        gather(False)

    for p in range(len(PIECES)):
        for sx in range(2):
            for sy in range(2):
                for sz in range(4):
                    copy(p, sx, sy, sz, 1 - core, mate, pass_sem.at[p], got_sem.at[p, sx, sy, sz]).wait_recv()

    for half in range(2):
        rows[0, :, half * HALF:(half + 1) * HALF] = reach[half, pl.ds(own_row, SLAB), :]

    def block(now, half, start):
        product = jnp.dot(rows[now], reach[half, :, start:start + 256], preferred_element_type=jnp.float32)
        old = rows[now, :, half * HALF + start:half * HALF + start + 256].astype(jnp.float32)
        return jnp.minimum(product + old, 1.0).astype(jnp.bfloat16)

    def two_steps(_, carry):
        for now in range(2):
            for half in range(2):
                for start in range(0, HALF, 256):
                    column = half * HALF + start
                    rows[1 - now, :, column:column + 256] = block(now, half, start)
        return carry

    lax.fori_loop(0, STEPS // 2, two_steps, 0)

    for half in range(2):
        @pl.when(y == half)
        def _():
            for start in range(0, HALF, 256):
                out_ref[:, start:start + 256] = block(0, half, start)


def solution(mesh):
    layout = P(('row', 'depth'), 'col')
    sends = len(PIECES)

    def local(slab):
        return pl.pallas_call(
            kernel,
            out_shape=jax.ShapeDtypeStruct((SLAB, HALF), jnp.bfloat16),
            in_specs=[pl.BlockSpec(memory_space=pl.ANY)],
            out_specs=pl.BlockSpec(memory_space=pltpu.VMEM),
            scratch_shapes=[
                pltpu.VMEM((2, N, HALF), jnp.bfloat16),
                pltpu.VMEM((2, SLAB, N), jnp.bfloat16),
                pltpu.SemaphoreType.DMA,
                pltpu.SemaphoreType.DMA((sends,)),
                pltpu.SemaphoreType.DMA((sends, 2, 2, 4)),
                pltpu.SemaphoreType.DMA((sends,)),
                pltpu.SemaphoreType.DMA((sends, 2, 2, 4)),
            ],
            compiler_params=pltpu.CompilerParams(collective_id=0, has_side_effects=True),
        )(slab)

    return jax.shard_map(local, mesh=mesh, in_specs=(layout,), out_specs=layout, check_vma=False)
```

time: 419 us -> 57.8 us (0.14)
  waiting for transfers between devices: 373 us -> 0 us
  Pallas kernels: 0 us -> 56 us
  between operations: 13.6 us -> 0.01 us
  starting transfers between devices: 11.1 us -> 0 us
  matrix products: 8.21 us -> 0 us
  other arithmetic: 7.25 us -> 0 us
    reduce_scatter x4 -> x0, waiting for transfers between devices: 259 us -> none  [local_squarings(): lax.psum_scatter(partial_sum, 'depth', scatter_dimension=0, tiled=True)]
    all_gather x4 -> x0, waiting for transfers between devices: 113 us -> none  [local_squarings(): full_block = lax.all_gather(row_slab, 'depth', axis=0, tiled=True)]
    pallas_call x0 -> x1, Pallas kernels: none -> 56 us  [local(): pl.pallas_call(kernel, out_shape=jax.ShapeDtypeStruct((SLAB, HALF), jnp.b...]
    ppermute x8 -> x0, starting transfers between devices: 10.8 us -> none  [the longest x4 7.48 us: local_squarings(): b_block = lax.ppermute(full_block, all_axes, b_skew)]
    dot_general x4 -> x0, matrix products: 8.21 us -> none  [local_squarings(): jnp.dot(window[slot_id], b_block, preferred_element_type=jnp.float32)]
    convert_element_type x4 -> x0, other arithmetic: 7.25 us -> none  [local_squarings(): jnp.minimum(reduced + row_slab.astype(jnp.float32), 1.0)]
    dynamic_slice x4 -> x0, local copies, waits for them, and re-layouts: 4.3 us -> none  [local_squarings(): lax.dynamic_slice_in_dim(full_block, sub_idx * k_width, k_width, axis=1)]
  transfers between devices with their start and end apart: 16 -> 0, of which waited for: 8 -> 0; matrix products, arithmetic and copies ran while one was open for 1% -> 0% of each run, Pallas kernels for 0% -> 0%
where the time goes in v1:
time: 57.8 us; the launch traced here: 57.7 us
  Pallas kernels  56 us (97%)
  local copies, waits for them, and re-layouts  1.67 us (3%)
    pallas_call x1, Pallas kernels, local(): pl.pallas_call(kernel, out_shape=jax.ShapeDtypeStruct((SLAB, HALF), jnp.b...  56 us
    unnamed x1, local copies, waits for them, and re-layouts  1.67 us

profile of v1, /device:TPU:0, one launch (start us, length us, event | category | flops | bytes accessed | tf_op | source)
XLA Modules:
  0.0 57.7 jit_solution(9599589880342546671)
XLA Ops:
  0.0 56.0 %shard_map.17 = bf16[128,1024]{1,0:T(8,128)(2,1)} custom-call(bf16[128,1024]{1,0:T(8,128)(2,1)} %in_ref.1), custom_call_target="tpu_custom_call" | custom-call | tf_op jit(solution)/shard_map/pallas_call | solution.py:170
  56.0 1.7 %copy.3 = bf16[128,1024]{1,0:T(8,128)(2,1)} copy(bf16[128,1024]{1,0:T(8,128)(2,1)} %shard_map.17) | data formatting | bytes 524288

commit v2 on v1

--- a/solution.py
+++ b/solution.py
@@ -169,7 +169,7 @@
     def local(slab):
         return pl.pallas_call(
             kernel,
-            out_shape=jax.ShapeDtypeStruct((SLAB, HALF), jnp.bfloat16),
+            out_shape=pltpu.VMEM((SLAB, HALF), jnp.bfloat16),
             in_specs=[pl.BlockSpec(memory_space=pl.ANY)],
             out_specs=pl.BlockSpec(memory_space=pltpu.VMEM),
             scratch_shapes=[

time: 57.8 us -> 56.2 us (0.972)
  local copies, waits for them, and re-layouts: 1.67 us -> 0.71 us
  Pallas kernels: 56 us -> 55.3 us
    unnamed x1, local copies, waits for them, and re-layouts: 1.67 us -> 0.71 us
    pallas_call x1, Pallas kernels: 56 us -> 55.3 us  [local(): pl.pallas_call(kernel, out_shape=pltpu.VMEM((SLAB, HALF), jnp.bfloat16),...]
where the time goes in v2:
time: 56.2 us; the launch traced here: 56 us
  Pallas kernels  55.3 us (98%)
  local copies, waits for them, and re-layouts  0.71 us (1%)
    pallas_call x1, Pallas kernels, local(): pl.pallas_call(kernel, out_shape=pltpu.VMEM((SLAB, HALF), jnp.bfloat16),...  55.3 us

profile of v2, /device:TPU:0, one launch (start us, length us, event | category | flops | bytes accessed | tf_op | source)
XLA Modules:
  0.0 56.0 jit_solution(4667708952460373463)
XLA Ops:
  0.0 55.3 %shard_map.17 = bf16[128,1024]{1,0:T(8,128)(2,1)S(1)} custom-call(bf16[128,1024]{1,0:T(8,128)(2,1)} %in_ref.1), custom_call_target="tpu_custom_call" | custom-call | tf_op jit(solution)/shard_map/pallas_call | solution.py:170
  55.3 0.7 %copy.3 = bf16[128,1024]{1,0:T(8,128)(2,1)} copy(bf16[128,1024]{1,0:T(8,128)(2,1)S(1)} %shard_map.17) | data formatting | bytes 524288

commit v3 on v2

--- a/solution.py
+++ b/solution.py
@@ -11,14 +11,26 @@
 STEPS = 15
 MESH = pl.DeviceIdType.MESH
 
-PIECES = (('zxy', 0, 48), ('zyx', 48, 48), ('xyz', 96, 16), ('yxz', 112, 16))
+PIECES = (
+    ('zxy', 0, 32, 0, 1024),
+    ('zxy', 96, 32, 0, 128),
+    ('zyx', 32, 32, 0, 1024),
+    ('zyx', 64, 16, 0, 1024),
+    ('zxy', 80, 16, 0, 1024),
+    ('xyz', 96, 16, 128, 896),
+    ('yxz', 112, 16, 128, 896),
+)
 END_ORDER = (
-    1, 4, 8, 17, 20, 24, 33, 36, 40, 49, 52, 56, 2, 9, 5, 12, 18, 25, 28, 34, 37, 41, 21, 44, 60, 57, 50, 53, 10, 6,
-    13, 3, 26, 19, 22, 29, 35, 38, 42, 58, 14, 11, 51, 54, 7, 27, 39, 43, 55, 59, 23, 30, 45, 61, 47, 15, 63, 46, 62, 31,
+    1, 4, 8, 17, 20, 24, 33, 36, 40, 49, 52, 56, 65, 68, 72, 81, 84, 88, 97, 100, 104, 2, 9, 18, 25, 5, 12, 34, 21,
+    28, 50, 41, 44, 66, 37, 53, 57, 60, 82, 85, 89, 69, 76, 73, 108, 92, 98, 101, 105, 10, 26, 6, 13, 3, 19, 42, 22,
+    29, 58, 35, 74, 51, 38, 67, 54, 45, 70, 61, 83, 86, 90, 77, 11, 27, 14, 99, 102, 30, 106, 43, 7, 87, 91, 23, 59,
+    103, 107, 39, 46, 78, 109, 75, 93, 55, 62, 111, 71, 95, 110, 15, 31, 47, 94, 79, 63,
 )
 MID_ORDER = (
-    1, 2, 4, 8, 17, 18, 20, 24, 33, 34, 36, 40, 49, 50, 52, 56, 3, 37, 41, 9, 10, 53, 57, 5, 6, 19, 12, 35, 38, 42,
-    58, 51, 54, 25, 26, 28, 21, 22, 39, 43, 45, 61, 55, 59, 44, 60, 7, 11, 47, 63, 46, 27, 62, 13, 14, 29, 30, 23, 15, 31,
+    1, 2, 4, 8, 17, 18, 20, 24, 33, 34, 36, 40, 49, 50, 52, 56, 65, 66, 68, 72, 81, 82, 84, 88, 97, 98, 100, 104, 3,
+    19, 9, 10, 85, 89, 5, 6, 12, 35, 25, 26, 51, 101, 105, 67, 21, 22, 28, 83, 86, 90, 41, 42, 44, 37, 38, 99, 102,
+    106, 53, 54, 60, 57, 58, 87, 91, 109, 103, 107, 76, 69, 70, 73, 74, 93, 108, 92, 11, 111, 27, 95, 7, 110, 43,
+    23, 13, 14, 94, 59, 75, 29, 30, 39, 45, 46, 55, 71, 61, 62, 77, 78, 47, 15, 63, 31, 79,
 )
 
 
@@ -79,8 +91,9 @@
 
     def piece_ref(p, sx, sy, sz, score):
         half, block = slab_at(sx, sy, sz, score)
-        start = pl.multiple_of(block * SLAB + PIECES[p][1], 16)
-        return reach.at[half, pl.ds(start, PIECES[p][2]), :]
+        _, first, count, column, width = PIECES[p]
+        start = pl.multiple_of(block * SLAB + first, 16)
+        return reach.at[half, pl.ds(start, count), pl.ds(column, width)]
 
     def copy(p, sx, sy, sz, score, peer, send, recv):
         ref = piece_ref(p, sx, sy, sz, score)

time: 56.2 us -> 56.6 us (level)
  no operation moved by 1% of the time
where the time goes in v3:
time: 56.6 us; the launch traced here: 56.4 us
  Pallas kernels  55.7 us (98%)
  local copies, waits for them, and re-layouts  0.71 us (1%)
    pallas_call x1, Pallas kernels, local(): pl.pallas_call(kernel, out_shape=pltpu.VMEM((SLAB, HALF), jnp.bfloat16),...  55.7 us

profile of v3, /device:TPU:0, one launch (start us, length us, event | category | flops | bytes accessed | tf_op | source)
XLA Modules:
  0.0 56.4 jit_solution(11909041288934452708)
XLA Ops:
  0.0 55.7 %shard_map.17 = bf16[128,1024]{1,0:T(8,128)(2,1)S(1)} custom-call(bf16[128,1024]{1,0:T(8,128)(2,1)} %in_ref.1), custom_call_target="tpu_custom_call" | custom-call | tf_op jit(solution)/shard_map/pallas_call | solution.py:183
  55.7 0.7 %copy.3 = bf16[128,1024]{1,0:T(8,128)(2,1)} copy(bf16[128,1024]{1,0:T(8,128)(2,1)S(1)} %shard_map.17) | data formatting | bytes 524288

commit v4 on v2

--- a/solution.py
+++ b/solution.py
@@ -11,14 +11,14 @@
 STEPS = 15
 MESH = pl.DeviceIdType.MESH
 
-PIECES = (('zxy', 0, 48), ('zyx', 48, 48), ('xyz', 96, 16), ('yxz', 112, 16))
+PIECES = (('zxy', 0, 48), ('zyx', 48, 48), ('yxz', 96, 32))
 END_ORDER = (
-    1, 4, 8, 17, 20, 24, 33, 36, 40, 49, 52, 56, 2, 9, 5, 12, 18, 25, 28, 34, 37, 41, 21, 44, 60, 57, 50, 53, 10, 6,
-    13, 3, 26, 19, 22, 29, 35, 38, 42, 58, 14, 11, 51, 54, 7, 27, 39, 43, 55, 59, 23, 30, 45, 61, 47, 15, 63, 46, 62, 31,
+    8, 4, 1, 24, 20, 17, 40, 36, 33, 9, 2, 12, 5, 18, 28, 25, 21, 41, 37, 34, 44, 13, 6, 10, 3, 26, 22, 19, 29, 35,
+    14, 38, 42, 11, 7, 30, 23, 43, 39, 27, 45, 15, 47, 31, 46,
 )
 MID_ORDER = (
-    1, 2, 4, 8, 17, 18, 20, 24, 33, 34, 36, 40, 49, 50, 52, 56, 3, 37, 41, 9, 10, 53, 57, 5, 6, 19, 12, 35, 38, 42,
-    58, 51, 54, 25, 26, 28, 21, 22, 39, 43, 45, 61, 55, 59, 44, 60, 7, 11, 47, 63, 46, 27, 62, 13, 14, 29, 30, 23, 15, 31,
+    1, 8, 4, 2, 17, 24, 20, 18, 33, 40, 36, 34, 3, 9, 10, 5, 41, 37, 19, 6, 12, 35, 38, 42, 25, 26, 28, 21, 22, 39,
+    43, 45, 44, 7, 11, 47, 13, 14, 27, 46, 23, 29, 30, 15, 31,
 )
 
 

time: 56.2 us -> 54.8 us (0.975)
  Pallas kernels: 55.3 us -> 53.9 us
    pallas_call x1, Pallas kernels: 55.3 us -> 53.9 us  [local(): pl.pallas_call(kernel, out_shape=pltpu.VMEM((SLAB, HALF), jnp.bfloat16),...]
where the time goes in v4:
time: 54.8 us; the launch traced here: 54.6 us
  Pallas kernels  53.9 us (98%)
  local copies, waits for them, and re-layouts  0.71 us (1%)
    pallas_call x1, Pallas kernels, local(): pl.pallas_call(kernel, out_shape=pltpu.VMEM((SLAB, HALF), jnp.bfloat16),...  53.9 us

profile of v4, /device:TPU:0, one launch (start us, length us, event | category | flops | bytes accessed | tf_op | source)
XLA Modules:
  0.0 54.6 jit_solution(13924332461540632316)
XLA Ops:
  0.0 53.9 %shard_map.17 = bf16[128,1024]{1,0:T(8,128)(2,1)S(1)} custom-call(bf16[128,1024]{1,0:T(8,128)(2,1)} %in_ref.1), custom_call_target="tpu_custom_call" | custom-call | tf_op jit(solution)/shard_map/pallas_call | solution.py:170
  53.9 0.7 %copy.3 = bf16[128,1024]{1,0:T(8,128)(2,1)} copy(bf16[128,1024]{1,0:T(8,128)(2,1)S(1)} %shard_map.17) | data formatting | bytes 524288

commit v5 on v4

--- a/solution.py
+++ b/solution.py
@@ -20,6 +20,9 @@
     1, 8, 4, 2, 17, 24, 20, 18, 33, 40, 36, 34, 3, 9, 10, 5, 41, 37, 19, 6, 12, 35, 38, 42, 25, 26, 28, 21, 22, 39,
     43, 45, 44, 7, 11, 47, 13, 14, 27, 46, 23, 29, 30, 15, 31,
 )
+
+END_GROUPS = ((10, (0, 1, 8, 4)), (24, (2, 9, 5, 12)), (36, (3, 10, 6)), (42, (11, 7, 13)), (44, (14, 15)))
+MID_GROUPS = ((13, (0, 1, 8, 2, 4)), (29, (3, 9)), (34, (10, 5, 6, 12)), (43, (11, 7, 13)), (44, (14, 15)))
 
 
 def forwards(order, dx, dy, k, end):
@@ -36,7 +39,7 @@
     return hops
 
 
-def kernel(in_ref, out_ref, reach, rows, in_sem, send_sem, recv_sem, pass_sem, got_sem):
+def kernel(in_ref, out_ref, reach, rows, total, in_sem, send_sem, recv_sem, pass_sem, got_sem):
     z, y, row = lax.axis_index('depth'), lax.axis_index('col'), lax.axis_index('row')
     x, core = row // 2, row % 2
     upper = z >= 2
@@ -108,20 +111,57 @@
                 copy(p, sx, sy, sz, core, peers[hop], send_sem.at[p], recv_sem.at[p, sx, sy, sz]).start()
             copy(p, sx, sy, sz, core, mate, pass_sem.at[p], got_sem.at[p, sx, sy, sz]).start()
 
+        def first_product(units, fresh):
+            terms = {0: [], 1: []}
+            for unit in units:
+                dx, dy, k = unit // 8, unit // 4 % 2, unit % 4
+                sx, sy, sz = source(dx, dy, k)
+                for p in range(len(PIECES)):
+                    copy(p, sx, sy, sz, 1 - core, mate, pass_sem.at[p], got_sem.at[p, sx, sy, sz]).wait_recv()
+                left, right = [], []
+                for score in range(2):
+                    spot = pl.multiple_of((score * 4 + sz) * SLAB, SLAB)
+                    left.append(rows[0, sx, :, pl.ds(spot, SLAB)])
+                    right.append(pl.ds(pl.multiple_of(sx * HALF + spot, SLAB), SLAB))
+                terms[dy].append((jnp.concatenate(left, axis=1), right))
+            for dy in range(2):
+                if not terms[dy]:
+                    continue
+                half = (1 - y) if dy else y
+                left = jnp.concatenate([term[0] for term in terms[dy]], axis=1)
+                for start in range(0, HALF, 256):
+                    right = [reach[half, spot, start:start + 256] for term in terms[dy] for spot in term[1]]
+                    product = jnp.dot(left, jnp.concatenate(right, axis=0), preferred_element_type=jnp.float32)
+                    if fresh:
+                        total[half, :, start:start + 256] = product
+                    else:
+                        total[half, :, start:start + 256] += product
+
         for p in range(len(PIECES)):
             push(p, 0, 0, 0)
-        for code in END_ORDER if end_case else MID_ORDER:
+        rows[0, y] = reach[y, pl.ds(own_row, SLAB), :]
+        groups = dict(END_GROUPS if end_case else MID_GROUPS)
+        fresh = True
+        for place, code in enumerate(END_ORDER if end_case else MID_ORDER):
             p, dx, dy, k = code // 16, code // 8 % 2, code // 4 % 2, code % 4
             sx, sy, sz = source(dx, dy, k)
             copy(p, sx, sy, sz, core, mate, send_sem.at[p], recv_sem.at[p, sx, sy, sz]).wait_recv()
             push(p, dx, dy, k)
+            if place in groups:
+                if fresh:
+                    rows[0, 1 - y] = reach[1 - y, pl.ds(own_row, SLAB), :]
+                first_product(groups[place], fresh)
+                fresh = False
+
+        def drain(p, count, semaphore):
+            ref = reach.at[0, pl.ds(0, count * PIECES[p][2]), :]
+            pltpu.make_async_remote_copy(
+                src_ref=ref, dst_ref=ref, send_sem=semaphore, recv_sem=semaphore, device_id=mate, device_id_type=MESH
+            ).wait_send()
+
         for p in range(len(PIECES)):
-            drain = copy(p, x, y, z, core, mate, send_sem.at[p], got_sem.at[p, x, y, z])
-            for _ in range(sent[p]):
-                drain.wait_send()
-            drain = copy(p, x, y, z, core, mate, pass_sem.at[p], got_sem.at[p, x, y, z])
-            for _ in range(16):
-                drain.wait_send()
+            drain(p, sent[p], send_sem.at[p])
+            drain(p, 16, pass_sem.at[p])
 
     @pl.when(end)
     def _():
@@ -131,35 +171,36 @@
     def _():
         gather(False)
 
-    for p in range(len(PIECES)):
-        for sx in range(2):
-            for sy in range(2):
-                for sz in range(4):
-                    copy(p, sx, sy, sz, 1 - core, mate, pass_sem.at[p], got_sem.at[p, sx, sy, sz]).wait_recv()
-
     for half in range(2):
-        rows[0, :, half * HALF:(half + 1) * HALF] = reach[half, pl.ds(own_row, SLAB), :]
+        for start in range(0, HALF, 256):
+            part = (0, half, slice(None), slice(start, start + 256))
+            grown = total[half, :, start:start + 256] + rows[part].astype(jnp.float32)
+            rows[part] = jnp.minimum(grown, 1.0).astype(jnp.bfloat16)
 
     def block(now, half, start):
-        product = jnp.dot(rows[now], reach[half, :, start:start + 256], preferred_element_type=jnp.float32)
-        old = rows[now, :, half * HALF + start:half * HALF + start + 256].astype(jnp.float32)
+        known = jnp.concatenate([rows[now, 0], rows[now, 1]], axis=1)
+        product = jnp.dot(known, reach[half, :, start:start + 256], preferred_element_type=jnp.float32)
+        old = rows[now, half, :, start:start + 256].astype(jnp.float32)
         return jnp.minimum(product + old, 1.0).astype(jnp.bfloat16)
 
+    def step(now):
+        for half in range(2):
+            for start in range(0, HALF, 256):
+                rows[1 - now, half, :, start:start + 256] = block(now, half, start)
+
     def two_steps(_, carry):
-        for now in range(2):
-            for half in range(2):
-                for start in range(0, HALF, 256):
-                    column = half * HALF + start
-                    rows[1 - now, :, column:column + 256] = block(now, half, start)
+        step(0)
+        step(1)
         return carry
 
-    lax.fori_loop(0, STEPS // 2, two_steps, 0)
+    lax.fori_loop(0, (STEPS - 2) // 2, two_steps, 0)
+    step(0)
 
     for half in range(2):
         @pl.when(y == half)
         def _():
             for start in range(0, HALF, 256):
-                out_ref[:, start:start + 256] = block(0, half, start)
+                out_ref[:, start:start + 256] = block(1, half, start)
 
 
 def solution(mesh):
@@ -174,7 +215,8 @@
             out_specs=pl.BlockSpec(memory_space=pltpu.VMEM),
             scratch_shapes=[
                 pltpu.VMEM((2, N, HALF), jnp.bfloat16),
-                pltpu.VMEM((2, SLAB, N), jnp.bfloat16),
+                pltpu.VMEM((2, 2, SLAB, HALF), jnp.bfloat16),
+                pltpu.VMEM((2, SLAB, HALF), jnp.float32),
                 pltpu.SemaphoreType.DMA,
                 pltpu.SemaphoreType.DMA((sends,)),
                 pltpu.SemaphoreType.DMA((sends, 2, 2, 4)),

time: 54.8 us -> 53.8 us (0.982)
  Pallas kernels: 53.9 us -> 53 us
    pallas_call x1, Pallas kernels: 53.9 us -> 53 us  [local(): pl.pallas_call(kernel, out_shape=pltpu.VMEM((SLAB, HALF), jnp.bfloat16),...]
where the time goes in v5:
time: 53.8 us; the launch traced here: 53.7 us
  Pallas kernels  53 us (99%)
  local copies, waits for them, and re-layouts  0.71 us (1%)
    pallas_call x1, Pallas kernels, local(): pl.pallas_call(kernel, out_shape=pltpu.VMEM((SLAB, HALF), jnp.bfloat16),...  53 us

profile of v5, /device:TPU:0, one launch (start us, length us, event | category | flops | bytes accessed | tf_op | source)
XLA Modules:
  0.0 53.7 jit_solution(16387068118497179100)
XLA Ops:
  0.0 53.0 %shard_map.17 = bf16[128,1024]{1,0:T(8,128)(2,1)S(1)} custom-call(bf16[128,1024]{1,0:T(8,128)(2,1)} %in_ref.1), custom_call_target="tpu_custom_call" | custom-call | tf_op jit(solution)/shard_map/pallas_call | solution.py:211
  53.0 0.7 %copy.3 = bf16[128,1024]{1,0:T(8,128)(2,1)} copy(bf16[128,1024]{1,0:T(8,128)(2,1)S(1)} %shard_map.17) | data formatting | bytes 524288

commit v6 on v5

--- a/solution.py
+++ b/solution.py
@@ -177,16 +177,16 @@
             grown = total[half, :, start:start + 256] + rows[part].astype(jnp.float32)
             rows[part] = jnp.minimum(grown, 1.0).astype(jnp.bfloat16)
 
-    def block(now, half, start):
+    def block(now, half, start, width=256):
         known = jnp.concatenate([rows[now, 0], rows[now, 1]], axis=1)
-        product = jnp.dot(known, reach[half, :, start:start + 256], preferred_element_type=jnp.float32)
-        old = rows[now, half, :, start:start + 256].astype(jnp.float32)
+        product = jnp.dot(known, reach[half, :, start:start + width], preferred_element_type=jnp.float32)
+        old = rows[now, half, :, start:start + width].astype(jnp.float32)
         return jnp.minimum(product + old, 1.0).astype(jnp.bfloat16)
 
     def step(now):
         for half in range(2):
-            for start in range(0, HALF, 256):
-                rows[1 - now, half, :, start:start + 256] = block(now, half, start)
+            for start in range(0, HALF, 1024):
+                rows[1 - now, half, :, start:start + 1024] = block(now, half, start, 1024)
 
     def two_steps(_, carry):
         step(0)

time: 53.8 us -> 53.8 us (level)
  no operation moved by 1% of the time
where the time goes in v6:
time: 53.8 us; the launch traced here: 53.7 us
  Pallas kernels  53 us (99%)
  local copies, waits for them, and re-layouts  0.71 us (1%)
    pallas_call x1, Pallas kernels, local(): pl.pallas_call(kernel, out_shape=pltpu.VMEM((SLAB, HALF), jnp.bfloat16),...  53 us

profile of v6, /device:TPU:0, one launch (start us, length us, event | category | flops | bytes accessed | tf_op | source)
XLA Modules:
  0.0 53.7 jit_solution(7733480318050586171)
XLA Ops:
  0.0 53.0 %shard_map.17 = bf16[128,1024]{1,0:T(8,128)(2,1)S(1)} custom-call(bf16[128,1024]{1,0:T(8,128)(2,1)} %in_ref.1), custom_call_target="tpu_custom_call" | custom-call | tf_op jit(solution)/shard_map/pallas_call | solution.py:211
  53.0 0.7 %copy.3 = bf16[128,1024]{1,0:T(8,128)(2,1)} copy(bf16[128,1024]{1,0:T(8,128)(2,1)S(1)} %shard_map.17) | data formatting | bytes 524288

commit v7 on v6

--- a/solution.py
+++ b/solution.py
@@ -8,6 +8,9 @@
 N = 2048
 SLAB = 128
 HALF = 1024
+TILES = 8
+WIDTH = 4
+PAD = 16
 STEPS = 15
 MESH = pl.DeviceIdType.MESH
 
@@ -61,8 +64,14 @@
 
     own_half, own_block = slab_at(x, y, z, core)
     own_row = pl.multiple_of(own_block * SLAB, SLAB)
-    load = pltpu.make_async_copy(in_ref, reach.at[own_half, pl.ds(own_row, SLAB), :], in_sem)
-    load.start()
+    loads = [
+        pltpu.make_async_copy(
+            in_ref.at[:, i * SLAB:(i + 1) * SLAB], reach.at[own_half * TILES + i, pl.ds(own_row, SLAB), :], in_sem.at[i]
+        )
+        for i in range(TILES)
+    ]
+    for load in loads:
+        load.start()
 
     barrier = pltpu.get_barrier_semaphore()
     for name in ('x', 'y', 'in'):
@@ -78,12 +87,13 @@
     def _():
         pl.semaphore_wait(barrier, 4)
 
-    load.wait()
+    for load in loads:
+        load.wait()
 
     def piece_ref(p, sx, sy, sz, score):
         half, block = slab_at(sx, sy, sz, score)
         start = pl.multiple_of(block * SLAB + PIECES[p][1], 16)
-        return reach.at[half, pl.ds(start, PIECES[p][2]), :]
+        return reach.at[pl.ds(half * TILES, TILES), pl.ds(start, PIECES[p][2]), :]
 
     def copy(p, sx, sy, sz, score, peer, send, recv):
         ref = piece_ref(p, sx, sy, sz, score)
@@ -118,28 +128,31 @@
                 sx, sy, sz = source(dx, dy, k)
                 for p in range(len(PIECES)):
                     copy(p, sx, sy, sz, 1 - core, mate, pass_sem.at[p], got_sem.at[p, sx, sy, sz]).wait_recv()
-                left, right = [], []
-                for score in range(2):
-                    spot = pl.multiple_of((score * 4 + sz) * SLAB, SLAB)
-                    left.append(rows[0, sx, :, pl.ds(spot, SLAB)])
-                    right.append(pl.ds(pl.multiple_of(sx * HALF + spot, SLAB), SLAB))
-                terms[dy].append((jnp.concatenate(left, axis=1), right))
+                blocks = [(sx * 2 + score) * 4 + sz for score in range(2)]
+                left = jnp.concatenate([rows[0, spot] for spot in blocks], axis=1)
+                terms[dy].append((left, [pl.ds(pl.multiple_of(spot * SLAB, SLAB), SLAB) for spot in blocks]))
             for dy in range(2):
                 if not terms[dy]:
                     continue
-                half = (1 - y) if dy else y
+                first = ((1 - y) if dy else y) * TILES
                 left = jnp.concatenate([term[0] for term in terms[dy]], axis=1)
-                for start in range(0, HALF, 256):
-                    right = [reach[half, spot, start:start + 256] for term in terms[dy] for spot in term[1]]
+                for i in range(0, TILES, 2):
+                    right = [
+                        jnp.concatenate([reach[first + i, spot], reach[first + i + 1, spot]], axis=1)
+                        for term in terms[dy] for spot in term[1]
+                    ]
                     product = jnp.dot(left, jnp.concatenate(right, axis=0), preferred_element_type=jnp.float32)
-                    if fresh:
-                        total[half, :, start:start + 256] = product
-                    else:
-                        total[half, :, start:start + 256] += product
+                    for n in range(2):
+                        part = product[:, n * SLAB:(n + 1) * SLAB]
+                        total[first + i + n] = part if fresh else total[first + i + n] + part
 
         for p in range(len(PIECES)):
             push(p, 0, 0, 0)
-        rows[0, y] = reach[y, pl.ds(own_row, SLAB), :]
+        def own(half):
+            for i in range(TILES):
+                rows[0, half * TILES + i] = reach[half * TILES + i, pl.ds(own_row, SLAB), :]
+
+        own(y)
         groups = dict(END_GROUPS if end_case else MID_GROUPS)
         fresh = True
         for place, code in enumerate(END_ORDER if end_case else MID_ORDER):
@@ -149,12 +162,12 @@
             push(p, dx, dy, k)
             if place in groups:
                 if fresh:
-                    rows[0, 1 - y] = reach[1 - y, pl.ds(own_row, SLAB), :]
+                    own(1 - y)
                 first_product(groups[place], fresh)
                 fresh = False
 
         def drain(p, count, semaphore):
-            ref = reach.at[0, pl.ds(0, count * PIECES[p][2]), :]
+            ref = reach.at[pl.ds(0, TILES), pl.ds(0, count * PIECES[p][2]), :]
             pltpu.make_async_remote_copy(
                 src_ref=ref, dst_ref=ref, send_sem=semaphore, recv_sem=semaphore, device_id=mate, device_id_type=MESH
             ).wait_send()
@@ -171,22 +184,25 @@
     def _():
         gather(False)
 
-    for half in range(2):
-        for start in range(0, HALF, 256):
-            part = (0, half, slice(None), slice(start, start + 256))
-            grown = total[half, :, start:start + 256] + rows[part].astype(jnp.float32)
-            rows[part] = jnp.minimum(grown, 1.0).astype(jnp.bfloat16)
-
-    def block(now, half, start, width=256):
-        known = jnp.concatenate([rows[now, 0], rows[now, 1]], axis=1)
-        product = jnp.dot(known, reach[half, :, start:start + width], preferred_element_type=jnp.float32)
-        old = rows[now, half, :, start:start + width].astype(jnp.float32)
-        return jnp.minimum(product + old, 1.0).astype(jnp.bfloat16)
+    def capped(sums, old):
+        return jnp.minimum(sums + old.astype(jnp.float32), 1.0).astype(jnp.bfloat16)
+
+    for g in range(2 * TILES):
+        rows[0, g] = capped(total[g], rows[0, g])
+
+    def block(now, first, put):
+        known = jnp.concatenate([rows[now, g] for g in range(2 * TILES)], axis=1)
+        right = jnp.concatenate([reach[first + i, 0:N] for i in range(WIDTH)], axis=1)
+        product = jnp.dot(known, right, preferred_element_type=jnp.float32)
+        for i in range(WIDTH):
+            put(i, capped(product[:, i * SLAB:(i + 1) * SLAB], rows[now, first + i]))
 
     def step(now):
-        for half in range(2):
-            for start in range(0, HALF, 1024):
-                rows[1 - now, half, :, start:start + 1024] = block(now, half, start, 1024)
+        for first in range(0, 2 * TILES, WIDTH):
+            def put(i, value):
+                rows[1 - now, first + i] = value
+
+            block(now, first, put)
 
     def two_steps(_, carry):
         step(0)
@@ -196,11 +212,11 @@
     lax.fori_loop(0, (STEPS - 2) // 2, two_steps, 0)
     step(0)
 
-    for half in range(2):
-        @pl.when(y == half)
-        def _():
-            for start in range(0, HALF, 256):
-                out_ref[:, start:start + 256] = block(1, half, start)
+    for start in range(0, TILES, WIDTH):
+        def put(i, value):
+            out_ref[:, (start + i) * SLAB:(start + i + 1) * SLAB] = value
+
+        block(1, y * TILES + start, put)
 
 
 def solution(mesh):
@@ -214,10 +230,10 @@
             in_specs=[pl.BlockSpec(memory_space=pl.ANY)],
             out_specs=pl.BlockSpec(memory_space=pltpu.VMEM),
             scratch_shapes=[
-                pltpu.VMEM((2, N, HALF), jnp.bfloat16),
-                pltpu.VMEM((2, 2, SLAB, HALF), jnp.bfloat16),
-                pltpu.VMEM((2, SLAB, HALF), jnp.float32),
-                pltpu.SemaphoreType.DMA,
+                pltpu.VMEM((2 * TILES, N + PAD, SLAB), jnp.bfloat16),
+                pltpu.VMEM((2, 2 * TILES, SLAB, SLAB), jnp.bfloat16),
+                pltpu.VMEM((2 * TILES, SLAB, SLAB), jnp.float32),
+                pltpu.SemaphoreType.DMA((TILES,)),
                 pltpu.SemaphoreType.DMA((sends,)),
                 pltpu.SemaphoreType.DMA((sends, 2, 2, 4)),
                 pltpu.SemaphoreType.DMA((sends,)),

time: 53.8 us -> 56.2 us (1.045)
  Pallas kernels: 53 us -> 55.3 us
    pallas_call x1, Pallas kernels: 53 us -> 55.3 us  [local(): pl.pallas_call(kernel, out_shape=pltpu.VMEM((SLAB, HALF), jnp.bfloat16),...]
where the time goes in v7:
time: 56.2 us; the launch traced here: 56 us
  Pallas kernels  55.3 us (98%)
  local copies, waits for them, and re-layouts  0.71 us (1%)
    pallas_call x1, Pallas kernels, local(): pl.pallas_call(kernel, out_shape=pltpu.VMEM((SLAB, HALF), jnp.bfloat16),...  55.3 us

profile of v7, /device:TPU:0, one launch (start us, length us, event | category | flops | bytes accessed | tf_op | source)
XLA Modules:
  0.0 56.0 jit_solution(7606754478869129440)
XLA Ops:
  0.0 55.3 %shard_map.17 = bf16[128,1024]{1,0:T(8,128)(2,1)S(1)} custom-call(bf16[128,1024]{1,0:T(8,128)(2,1)} %in_ref.1), custom_call_target="tpu_custom_call" | custom-call | tf_op jit(solution)/shard_map/pallas_call | solution.py:227
  55.3 0.7 %copy.3 = bf16[128,1024]{1,0:T(8,128)(2,1)} copy(bf16[128,1024]{1,0:T(8,128)(2,1)S(1)} %shard_map.17) | data formatting | bytes 524288

commit v8 on v7

--- a/solution.py
+++ b/solution.py
@@ -10,7 +10,8 @@
 HALF = 1024
 TILES = 8
 WIDTH = 4
-PAD = 16
+GROUP = 16
+GROUPS = SLAB // GROUP
 STEPS = 15
 MESH = pl.DeviceIdType.MESH
 
@@ -63,10 +64,9 @@
         return sy, (sx * 2 + score) * 4 + sz
 
     own_half, own_block = slab_at(x, y, z, core)
-    own_row = pl.multiple_of(own_block * SLAB, SLAB)
     loads = [
         pltpu.make_async_copy(
-            in_ref.at[:, i * SLAB:(i + 1) * SLAB], reach.at[own_half * TILES + i, pl.ds(own_row, SLAB), :], in_sem.at[i]
+            in_ref.at[:, :, i * SLAB:(i + 1) * SLAB], reach.at[own_half, pl.ds(own_block * GROUPS, GROUPS), i], in_sem.at[i]
         )
         for i in range(TILES)
     ]
@@ -92,14 +92,17 @@
 
     def piece_ref(p, sx, sy, sz, score):
         half, block = slab_at(sx, sy, sz, score)
-        start = pl.multiple_of(block * SLAB + PIECES[p][1], 16)
-        return reach.at[pl.ds(half * TILES, TILES), pl.ds(start, PIECES[p][2]), :]
+        _, first, count = PIECES[p]
+        return reach.at[half, pl.ds(block * GROUPS + first // GROUP, count // GROUP)]
 
     def copy(p, sx, sy, sz, score, peer, send, recv):
         ref = piece_ref(p, sx, sy, sz, score)
         return pltpu.make_async_remote_copy(
             src_ref=ref, dst_ref=ref, send_sem=send, recv_sem=recv, device_id=peer, device_id_type=MESH
         )
+
+    def tile(half, block, i):
+        return reach[half, pl.ds(block * GROUPS, GROUPS), i].reshape(SLAB, SLAB)
 
     def gather(end_case):
         places = (0, 1, 2, 3) if end_case else (1, 0, 2, 3)
@@ -130,27 +133,28 @@
                     copy(p, sx, sy, sz, 1 - core, mate, pass_sem.at[p], got_sem.at[p, sx, sy, sz]).wait_recv()
                 blocks = [(sx * 2 + score) * 4 + sz for score in range(2)]
                 left = jnp.concatenate([rows[0, spot] for spot in blocks], axis=1)
-                terms[dy].append((left, [pl.ds(pl.multiple_of(spot * SLAB, SLAB), SLAB) for spot in blocks]))
+                terms[dy].append((left, blocks))
             for dy in range(2):
                 if not terms[dy]:
                     continue
-                first = ((1 - y) if dy else y) * TILES
+                half = (1 - y) if dy else y
                 left = jnp.concatenate([term[0] for term in terms[dy]], axis=1)
                 for i in range(0, TILES, 2):
                     right = [
-                        jnp.concatenate([reach[first + i, spot], reach[first + i + 1, spot]], axis=1)
+                        jnp.concatenate([tile(half, spot, i), tile(half, spot, i + 1)], axis=1)
                         for term in terms[dy] for spot in term[1]
                     ]
                     product = jnp.dot(left, jnp.concatenate(right, axis=0), preferred_element_type=jnp.float32)
                     for n in range(2):
                         part = product[:, n * SLAB:(n + 1) * SLAB]
-                        total[first + i + n] = part if fresh else total[first + i + n] + part
+                        g = half * TILES + i + n
+                        total[g] = part if fresh else total[g] + part
 
         for p in range(len(PIECES)):
             push(p, 0, 0, 0)
         def own(half):
             for i in range(TILES):
-                rows[0, half * TILES + i] = reach[half * TILES + i, pl.ds(own_row, SLAB), :]
+                rows[0, half * TILES + i] = tile(half, own_block, i)
 
         own(y)
         groups = dict(END_GROUPS if end_case else MID_GROUPS)
@@ -167,7 +171,7 @@
                 fresh = False
 
         def drain(p, count, semaphore):
-            ref = reach.at[pl.ds(0, TILES), pl.ds(0, count * PIECES[p][2]), :]
+            ref = reach.at[0, pl.ds(0, count * PIECES[p][2] // GROUP)]
             pltpu.make_async_remote_copy(
                 src_ref=ref, dst_ref=ref, send_sem=semaphore, recv_sem=semaphore, device_id=mate, device_id_type=MESH
             ).wait_send()
@@ -190,19 +194,20 @@
     for g in range(2 * TILES):
         rows[0, g] = capped(total[g], rows[0, g])
 
-    def block(now, first, put):
+    def block(now, half, first, put):
         known = jnp.concatenate([rows[now, g] for g in range(2 * TILES)], axis=1)
-        right = jnp.concatenate([reach[first + i, 0:N] for i in range(WIDTH)], axis=1)
+        right = jnp.concatenate([reach[half, :, first + i].reshape(N, SLAB) for i in range(WIDTH)], axis=1)
         product = jnp.dot(known, right, preferred_element_type=jnp.float32)
         for i in range(WIDTH):
-            put(i, capped(product[:, i * SLAB:(i + 1) * SLAB], rows[now, first + i]))
+            put(i, capped(product[:, i * SLAB:(i + 1) * SLAB], rows[now, half * TILES + first + i]))
 
     def step(now):
-        for first in range(0, 2 * TILES, WIDTH):
-            def put(i, value):
-                rows[1 - now, first + i] = value
-
-            block(now, first, put)
+        for half in range(2):
+            for first in range(0, TILES, WIDTH):
+                def put(i, value):
+                    rows[1 - now, half * TILES + first + i] = value
+
+                block(now, half, first, put)
 
     def two_steps(_, carry):
         step(0)
@@ -212,11 +217,11 @@
     lax.fori_loop(0, (STEPS - 2) // 2, two_steps, 0)
     step(0)
 
-    for start in range(0, TILES, WIDTH):
+    for first in range(0, TILES, WIDTH):
         def put(i, value):
-            out_ref[:, (start + i) * SLAB:(start + i + 1) * SLAB] = value
-
-        block(1, y * TILES + start, put)
+            out_ref[:, (first + i) * SLAB:(first + i + 1) * SLAB] = value
+
+        block(1, y, first, put)
 
 
 def solution(mesh):
@@ -230,7 +235,7 @@
             in_specs=[pl.BlockSpec(memory_space=pl.ANY)],
             out_specs=pl.BlockSpec(memory_space=pltpu.VMEM),
             scratch_shapes=[
-                pltpu.VMEM((2 * TILES, N + PAD, SLAB), jnp.bfloat16),
+                pltpu.VMEM((2, N // GROUP, TILES, GROUP, SLAB), jnp.bfloat16),
                 pltpu.VMEM((2, 2 * TILES, SLAB, SLAB), jnp.bfloat16),
                 pltpu.VMEM((2 * TILES, SLAB, SLAB), jnp.float32),
                 pltpu.SemaphoreType.DMA((TILES,)),
@@ -240,6 +245,6 @@
                 pltpu.SemaphoreType.DMA((sends, 2, 2, 4)),
             ],
             compiler_params=pltpu.CompilerParams(collective_id=0, has_side_effects=True),
-        )(slab)
+        )(slab.reshape(GROUPS, GROUP, HALF))
 
     return jax.shard_map(local, mesh=mesh, in_specs=(layout,), out_specs=layout, check_vma=False)

time: 56.2 us -> 56.2 us (level)
  no operation moved by 1% of the time
where the time goes in v8:
time: 56.2 us; the launch traced here: 56 us
  Pallas kernels  55.3 us (98%)
  local copies, waits for them, and re-layouts  0.71 us (1%)
    pallas_call x1, Pallas kernels, local(): pl.pallas_call(kernel, out_shape=pltpu.VMEM((SLAB, HALF), jnp.bfloat16),...  55.3 us

profile of v8, /device:TPU:0, one launch (start us, length us, event | category | flops | bytes accessed | tf_op | source)
XLA Modules:
  0.0 56.0 jit_solution(16319212407888424872)
XLA Ops:
  0.0 55.3 %shard_map.17 = bf16[128,1024]{1,0:T(8,128)(2,1)S(1)} custom-call(bf16[8,16,1024]{2,1,0:T(8,128)(2,1)} %bitcast.1), custom_call_target="tpu_custom_call" | custom-call | tf_op jit(solution)/shard_map/pallas_call | solution.py:232
  55.3 0.7 %copy.3 = bf16[128,1024]{1,0:T(8,128)(2,1)} copy(bf16[128,1024]{1,0:T(8,128)(2,1)S(1)} %shard_map.17) | data formatting | bytes 524288

commit v9 on v6

--- a/solution.py
+++ b/solution.py
@@ -185,22 +185,13 @@
 
     def step(now):
         for half in range(2):
-            for start in range(0, HALF, 1024):
-                rows[1 - now, half, :, start:start + 1024] = block(now, half, start, 1024)
-
-    def two_steps(_, carry):
-        step(0)
-        step(1)
-        return carry
-
-    lax.fori_loop(0, (STEPS - 2) // 2, two_steps, 0)
-    step(0)
-
-    for half in range(2):
-        @pl.when(y == half)
-        def _():
-            for start in range(0, HALF, 256):
-                out_ref[:, start:start + 256] = block(1, half, start)
+            rows[1 - now, half] = block(now, half, 0, HALF)
+
+    for count in range(STEPS - 2):
+        step(count % 2)
+
+    for start in range(0, HALF, 1024):
+        out_ref[:, start:start + 1024] = block(1, y, start, 1024)
 
 
 def solution(mesh):

time: 53.8 us -> 53 us (0.985)
  Pallas kernels: 53 us -> 52.1 us
    pallas_call x1, Pallas kernels: 53 us -> 52.1 us  [local(): pl.pallas_call(kernel, out_shape=pltpu.VMEM((SLAB, HALF), jnp.bfloat16),...]
where the time goes in v9:
time: 53 us; the launch traced here: 52.9 us
  Pallas kernels  52.1 us (98%)
  local copies, waits for them, and re-layouts  0.71 us (1%)
    pallas_call x1, Pallas kernels, local(): pl.pallas_call(kernel, out_shape=pltpu.VMEM((SLAB, HALF), jnp.bfloat16),...  52.1 us

profile of v9, /device:TPU:0, one launch (start us, length us, event | category | flops | bytes accessed | tf_op | source)
XLA Modules:
  0.0 52.9 jit_solution(8757937292170725476)
XLA Ops:
  0.0 52.1 %shard_map.17 = bf16[128,1024]{1,0:T(8,128)(2,1)S(1)} custom-call(bf16[128,1024]{1,0:T(8,128)(2,1)} %in_ref.1), custom_call_target="tpu_custom_call" | custom-call | tf_op jit(solution)/shard_map/pallas_call | solution.py:202
  52.1 0.7 %copy.3 = bf16[128,1024]{1,0:T(8,128)(2,1)} copy(bf16[128,1024]{1,0:T(8,128)(2,1)S(1)} %shard_map.17) | data formatting | bytes 524288

commit v10 on v9

--- a/solution.py
+++ b/solution.py
@@ -23,6 +23,8 @@
 
 END_GROUPS = ((10, (0, 1, 8, 4)), (24, (2, 9, 5, 12)), (36, (3, 10, 6)), (42, (11, 7, 13)), (44, (14, 15)))
 MID_GROUPS = ((13, (0, 1, 8, 2, 4)), (29, (3, 9)), (34, (10, 5, 6, 12)), (43, (11, 7, 13)), (44, (14, 15)))
+END_SECOND = 42
+MID_SECOND = 43
 
 
 def forwards(order, dx, dy, k, end):
@@ -39,7 +41,7 @@
     return hops
 
 
-def kernel(in_ref, out_ref, reach, rows, total, in_sem, send_sem, recv_sem, pass_sem, got_sem):
+def kernel(in_ref, out_ref, reach, rows, total, more, in_sem, send_sem, recv_sem, pass_sem, got_sem):
     z, y, row = lax.axis_index('depth'), lax.axis_index('col'), lax.axis_index('row')
     x, core = row // 2, row % 2
     upper = z >= 2
@@ -137,6 +139,44 @@
                     else:
                         total[half, :, start:start + 256] += product
 
+        def columns(sz, score):
+            return pl.ds(pl.multiple_of((score * 4 + sz) * SLAB, SLAB), SLAB)
+
+        def partial(places, start):
+            left, right = [], []
+            for k in places:
+                _, _, sz = source(0, 0, k)
+                for score in range(2):
+                    spot = columns(sz, score)
+                    left.append(rows[1, y, :, spot])
+                    first = pl.multiple_of(y * HALF + (score * 4 + sz) * SLAB, SLAB)
+                    right.append(reach[1 - y, pl.ds(first, SLAB), start:start + 256])
+            return jnp.dot(
+                jnp.concatenate(left, axis=1), jnp.concatenate(right, axis=0), preferred_element_type=jnp.float32
+            )
+
+        def second_product():
+            for start in range(0, HALF, 256):
+                grown = total[y, :, start:start + 256] + rows[0, y, :, start:start + 256].astype(jnp.float32)
+                rows[1, y, :, start:start + 256] = jnp.minimum(grown, 1.0).astype(jnp.bfloat16)
+            known = pl.ds(pl.multiple_of(y * HALF, HALF), HALF)
+            for start in range(0, HALF, 256):
+                more[y, :, start:start + 256] = jnp.dot(
+                    rows[1, y], reach[y, known, start:start + 256], preferred_element_type=jnp.float32
+                )
+
+            @pl.when(x == y)
+            def _():
+                for start in range(0, HALF, 256):
+                    more[1 - y, :, start:start + 256] = jnp.dot(
+                        rows[1, y], reach[1 - y, known, start:start + 256], preferred_element_type=jnp.float32
+                    )
+
+            @pl.when(x != y)
+            def _():
+                for start in range(0, HALF, 256):
+                    more[1 - y, :, start:start + 256] = partial((0, 1), start)
+
         for p in range(len(PIECES)):
             push(p, 0, 0, 0)
         rows[0, y] = reach[y, pl.ds(own_row, SLAB), :]
@@ -152,6 +192,13 @@
                     rows[0, 1 - y] = reach[1 - y, pl.ds(own_row, SLAB), :]
                 first_product(groups[place], fresh)
                 fresh = False
+            if place == (END_SECOND if end_case else MID_SECOND):
+                second_product()
+
+        @pl.when(x != y)
+        def _():
+            for start in range(0, HALF, 256):
+                more[1 - y, :, start:start + 256] += partial((2, 3), start)
 
         def drain(p, count, semaphore):
             ref = reach.at[0, pl.ds(0, count * PIECES[p][2]), :]
@@ -171,11 +218,18 @@
     def _():
         gather(False)
 
+    for start in range(0, HALF, 256):
+        grown = total[1 - y, :, start:start + 256] + rows[0, 1 - y, :, start:start + 256].astype(jnp.float32)
+        rows[1, 1 - y, :, start:start + 256] = jnp.minimum(grown, 1.0).astype(jnp.bfloat16)
+
+    known = pl.ds(pl.multiple_of((1 - y) * HALF, HALF), HALF)
     for half in range(2):
         for start in range(0, HALF, 256):
-            part = (0, half, slice(None), slice(start, start + 256))
-            grown = total[half, :, start:start + 256] + rows[part].astype(jnp.float32)
-            rows[part] = jnp.minimum(grown, 1.0).astype(jnp.bfloat16)
+            product = jnp.dot(
+                rows[1, 1 - y], reach[half, known, start:start + 256], preferred_element_type=jnp.float32
+            )
+            grown = product + more[half, :, start:start + 256] + rows[1, half, :, start:start + 256].astype(jnp.float32)
+            rows[0, half, :, start:start + 256] = jnp.minimum(grown, 1.0).astype(jnp.bfloat16)
 
     def block(now, half, start, width=256):
         known = jnp.concatenate([rows[now, 0], rows[now, 1]], axis=1)
@@ -187,11 +241,11 @@
         for half in range(2):
             rows[1 - now, half] = block(now, half, 0, HALF)
 
-    for count in range(STEPS - 2):
+    for count in range(STEPS - 3):
         step(count % 2)
 
     for start in range(0, HALF, 1024):
-        out_ref[:, start:start + 1024] = block(1, y, start, 1024)
+        out_ref[:, start:start + 1024] = block(0, y, start, 1024)
 
 
 def solution(mesh):
@@ -208,6 +262,7 @@
                 pltpu.VMEM((2, N, HALF), jnp.bfloat16),
                 pltpu.VMEM((2, 2, SLAB, HALF), jnp.bfloat16),
                 pltpu.VMEM((2, SLAB, HALF), jnp.float32),
+                pltpu.VMEM((2, SLAB, HALF), jnp.float32),
                 pltpu.SemaphoreType.DMA,
                 pltpu.SemaphoreType.DMA((sends,)),
                 pltpu.SemaphoreType.DMA((sends, 2, 2, 4)),

time: 53 us -> 53.5 us (level)
  Pallas kernels: 52.1 us -> 52.7 us
    pallas_call x1, Pallas kernels: 52.1 us -> 52.7 us  [local(): pl.pallas_call(kernel, out_shape=pltpu.VMEM((SLAB, HALF), jnp.bfloat16),...]
where the time goes in v10:
time: 53.5 us; the launch traced here: 53.4 us
  Pallas kernels  52.7 us (99%)
  local copies, waits for them, and re-layouts  0.71 us (1%)
    pallas_call x1, Pallas kernels, local(): pl.pallas_call(kernel, out_shape=pltpu.VMEM((SLAB, HALF), jnp.bfloat16),...  52.7 us

profile of v10, /device:TPU:0, one launch (start us, length us, event | category | flops | bytes accessed | tf_op | source)
XLA Modules:
  0.0 53.4 jit_solution(5619680533795295513)
XLA Ops:
  0.0 52.7 %shard_map.17 = bf16[128,1024]{1,0:T(8,128)(2,1)S(1)} custom-call(bf16[128,1024]{1,0:T(8,128)(2,1)} %in_ref.1), custom_call_target="tpu_custom_call" | custom-call | tf_op jit(solution)/shard_map/pallas_call | solution.py:256
  52.7 0.7 %copy.3 = bf16[128,1024]{1,0:T(8,128)(2,1)} copy(bf16[128,1024]{1,0:T(8,128)(2,1)S(1)} %shard_map.17) | data formatting | bytes 524288

commit v11 on v10

--- a/solution.py
+++ b/solution.py
@@ -21,9 +21,10 @@
     43, 45, 44, 7, 11, 47, 13, 14, 27, 46, 23, 29, 30, 15, 31,
 )
 
-END_GROUPS = ((10, (0, 1, 8, 4)), (24, (2, 9, 5, 12)), (36, (3, 10, 6)), (42, (11, 7, 13)), (44, (14, 15)))
-MID_GROUPS = ((13, (0, 1, 8, 2, 4)), (29, (3, 9)), (34, (10, 5, 6, 12)), (43, (11, 7, 13)), (44, (14, 15)))
-END_SECOND = 42
+END_GROUPS = ((10, (0, 1, 8, 4)), (24, (2, 9, 5, 12)), (36, (3, 10, 6)), (44, (11, 7, 13)))
+MID_GROUPS = ((13, (0, 1, 8, 2, 4)), (29, (3, 9)), (34, (10, 5, 6, 12)), (43, (11, 7, 13)))
+LAST_GROUP = (14, 15)
+END_SECOND = 44
 MID_SECOND = 43
 
 
@@ -195,6 +196,8 @@
             if place == (END_SECOND if end_case else MID_SECOND):
                 second_product()
 
+        first_product(LAST_GROUP, False)
+
         @pl.when(x != y)
         def _():
             for start in range(0, HALF, 256):

time: 53.5 us -> 53.1 us (level)
  no operation moved by 1% of the time
where the time goes in v11:
time: 53.1 us; the launch traced here: 53 us
  Pallas kernels  52.3 us (98%)
  local copies, waits for them, and re-layouts  0.71 us (1%)
    pallas_call x1, Pallas kernels, local(): pl.pallas_call(kernel, out_shape=pltpu.VMEM((SLAB, HALF), jnp.bfloat16),...  52.3 us

profile of v11, /device:TPU:0, one launch (start us, length us, event | category | flops | bytes accessed | tf_op | source)
XLA Modules:
  0.0 53.0 jit_solution(7320970226877634607)
XLA Ops:
  0.0 52.3 %shard_map.17 = bf16[128,1024]{1,0:T(8,128)(2,1)S(1)} custom-call(bf16[128,1024]{1,0:T(8,128)(2,1)} %in_ref.1), custom_call_target="tpu_custom_call" | custom-call | tf_op jit(solution)/shard_map/pallas_call | solution.py:259
  52.3 0.7 %copy.3 = bf16[128,1024]{1,0:T(8,128)(2,1)} copy(bf16[128,1024]{1,0:T(8,128)(2,1)S(1)} %shard_map.17) | data formatting | bytes 524288

commit v12 on v11

--- a/solution.py
+++ b/solution.py
@@ -21,10 +21,10 @@
     43, 45, 44, 7, 11, 47, 13, 14, 27, 46, 23, 29, 30, 15, 31,
 )
 
-END_GROUPS = ((10, (0, 1, 8, 4)), (24, (2, 9, 5, 12)), (36, (3, 10, 6)), (44, (11, 7, 13)))
+END_GROUPS = ((10, (0, 1, 8, 4)), (24, (2, 9, 5, 12)), (36, (3, 10, 6)), (41, (11, 7)), (43, (13,)))
 MID_GROUPS = ((13, (0, 1, 8, 2, 4)), (29, (3, 9)), (34, (10, 5, 6, 12)), (43, (11, 7, 13)))
 LAST_GROUP = (14, 15)
-END_SECOND = 44
+END_SECOND = 41
 MID_SECOND = 43
 
 
@@ -176,7 +176,7 @@
             @pl.when(x != y)
             def _():
                 for start in range(0, HALF, 256):
-                    more[1 - y, :, start:start + 256] = partial((0, 1), start)
+                    more[1 - y, :, start:start + 256] = partial((0,), start)
 
         for p in range(len(PIECES)):
             push(p, 0, 0, 0)
@@ -201,7 +201,7 @@
         @pl.when(x != y)
         def _():
             for start in range(0, HALF, 256):
-                more[1 - y, :, start:start + 256] += partial((2, 3), start)
+                more[1 - y, :, start:start + 256] += partial((1, 2, 3), start)
 
         def drain(p, count, semaphore):
             ref = reach.at[0, pl.ds(0, count * PIECES[p][2]), :]

time: 53.1 us -> 52.5 us (0.989)
  Pallas kernels: 52.3 us -> 51.6 us
    pallas_call x1, Pallas kernels: 52.3 us -> 51.6 us  [local(): pl.pallas_call(kernel, out_shape=pltpu.VMEM((SLAB, HALF), jnp.bfloat16),...]
where the time goes in v12:
time: 52.5 us; the launch traced here: 52.3 us
  Pallas kernels  51.6 us (98%)
  local copies, waits for them, and re-layouts  0.71 us (1%)
    pallas_call x1, Pallas kernels, local(): pl.pallas_call(kernel, out_shape=pltpu.VMEM((SLAB, HALF), jnp.bfloat16),...  51.6 us

profile of v12, /device:TPU:0, one launch (start us, length us, event | category | flops | bytes accessed | tf_op | source)
XLA Modules:
  0.0 52.3 jit_solution(7678642096044437457)
XLA Ops:
  0.0 51.6 %shard_map.17 = bf16[128,1024]{1,0:T(8,128)(2,1)S(1)} custom-call(bf16[128,1024]{1,0:T(8,128)(2,1)} %in_ref.1), custom_call_target="tpu_custom_call" | custom-call | tf_op jit(solution)/shard_map/pallas_call | solution.py:259
  51.6 0.7 %copy.3 = bf16[128,1024]{1,0:T(8,128)(2,1)} copy(bf16[128,1024]{1,0:T(8,128)(2,1)S(1)} %shard_map.17) | data formatting | bytes 524288

commit v13 on v12

--- a/solution.py
+++ b/solution.py
@@ -42,7 +42,7 @@
     return hops
 
 
-def kernel(in_ref, out_ref, reach, rows, total, more, in_sem, send_sem, recv_sem, pass_sem, got_sem):
+def kernel(in_ref, out_ref, reach, rows, total, more, in_sem, send_sem, recv_sem, pass_sem, got_sem, ready):
     z, y, row = lax.axis_index('depth'), lax.axis_index('col'), lax.axis_index('row')
     x, core = row // 2, row % 2
     upper = z >= 2
@@ -67,19 +67,29 @@
     load = pltpu.make_async_copy(in_ref, reach.at[own_half, pl.ds(own_row, SLAB), :], in_sem)
     load.start()
 
+    steps = (
+        (x == 0, x == 1, peers['x']),
+        (y == 0, y == 1, peers['y']),
+        (z < 3, None, {'depth': z + 1, 'col': y, 'row': row}),
+        (None, z > 0, {'depth': z - 1, 'col': y, 'row': row}),
+    )
     barrier = pltpu.get_barrier_semaphore()
-    for name in ('x', 'y', 'in'):
-        pl.semaphore_signal(barrier, inc=1, device_id=peers[name], device_id_type=MESH)
     pl.semaphore_signal(barrier, inc=1, device_id=mate, device_id_type=MESH)
-
-    @pl.when(jnp.logical_not(end))
-    def _():
-        pl.semaphore_signal(barrier, inc=1, device_id=peers['out'], device_id_type=MESH)
-        pl.semaphore_wait(barrier, 5)
-
-    @pl.when(end)
-    def _():
-        pl.semaphore_wait(barrier, 4)
+    for outwards, _, peer in steps:
+        if outwards is not None:
+            @pl.when(outwards)
+            def _():
+                pl.semaphore_signal(barrier, inc=1, device_id=peer, device_id_type=MESH)
+
+    pl.semaphore_wait(barrier, 1 + x + y + jnp.where(z > 0, 1, 0))
+    for _, inwards, peer in steps:
+        if inwards is not None:
+            @pl.when(inwards)
+            def _():
+                pl.semaphore_signal(ready, inc=1, device_id=peer, device_id_type=MESH)
+
+    is_inwards = {'x': x == 1, 'y': y == 1, 'in': upper, 'out': jnp.logical_not(upper)}
+    further = (1 - x) + (1 - y) + jnp.where(z < 3, 1, 0)
 
     load.wait()
 
@@ -178,8 +188,23 @@
                 for start in range(0, HALF, 256):
                     more[1 - y, :, start:start + 256] = partial((0,), start)
 
+        def first_push(inwards):
+            for p in range(len(PIECES)):
+                for hop in forwards(PIECES[p][0], 0, 0, 0, end_case):
+                    @pl.when(is_inwards[hop] if inwards else jnp.logical_not(is_inwards[hop]))
+                    def _():
+                        copy(p, x, y, z, core, peers[hop], send_sem.at[p], recv_sem.at[p, x, y, z]).start()
+
+        first_push(True)
         for p in range(len(PIECES)):
-            push(p, 0, 0, 0)
+            sent[p] += len(forwards(PIECES[p][0], 0, 0, 0, end_case))
+            copy(p, x, y, z, core, mate, pass_sem.at[p], got_sem.at[p, x, y, z]).start()
+
+        @pl.when(further > 0)
+        def _():
+            pl.semaphore_wait(ready, further)
+
+        first_push(False)
         rows[0, y] = reach[y, pl.ds(own_row, SLAB), :]
         groups = dict(END_GROUPS if end_case else MID_GROUPS)
         fresh = True
@@ -271,6 +296,7 @@
                 pltpu.SemaphoreType.DMA((sends, 2, 2, 4)),
                 pltpu.SemaphoreType.DMA((sends,)),
                 pltpu.SemaphoreType.DMA((sends, 2, 2, 4)),
+                pltpu.SemaphoreType.REGULAR,
             ],
             compiler_params=pltpu.CompilerParams(collective_id=0, has_side_effects=True),
         )(slab)

time: 52.5 us -> 52.1 us (level)
  Pallas kernels: 51.6 us -> 51 us
    pallas_call x1, Pallas kernels: 51.6 us -> 51 us  [local(): pl.pallas_call(kernel, out_shape=pltpu.VMEM((SLAB, HALF), jnp.bfloat16),...]
where the time goes in v13:
time: 52.1 us; the launch traced here: 51.7 us
  Pallas kernels  51 us (98%)
  local copies, waits for them, and re-layouts  0.71 us (1%)
    pallas_call x1, Pallas kernels, local(): pl.pallas_call(kernel, out_shape=pltpu.VMEM((SLAB, HALF), jnp.bfloat16),...  51 us

profile of v13, /device:TPU:0, one launch (start us, length us, event | category | flops | bytes accessed | tf_op | source)
XLA Modules:
  0.0 51.7 jit_solution(1162781968700531511)
XLA Ops:
  0.0 51.0 %shard_map.17 = bf16[128,1024]{1,0:T(8,128)(2,1)S(1)} custom-call(bf16[128,1024]{1,0:T(8,128)(2,1)} %in_ref.1), custom_call_target="tpu_custom_call" | custom-call | tf_op jit(solution)/shard_map/pallas_call | solution.py:284
  51.0 0.7 %copy.3 = bf16[128,1024]{1,0:T(8,128)(2,1)} copy(bf16[128,1024]{1,0:T(8,128)(2,1)S(1)} %shard_map.17) | data formatting | bytes 524288

commit v14 on v13

--- a/solution.py
+++ b/solution.py
@@ -104,6 +104,54 @@
             src_ref=ref, dst_ref=ref, send_sem=send, recv_sem=recv, device_id=peer, device_id_type=MESH
         )
 
+    def await_mate(units, source):
+        for unit in units:
+            sx, sy, sz = source(unit // 8, unit // 4 % 2, unit % 4)
+            for p in range(len(PIECES)):
+                copy(p, sx, sy, sz, 1 - core, mate, pass_sem.at[p], got_sem.at[p, sx, sy, sz]).wait_recv()
+
+    def first_product(units, fresh, source):
+        terms = {0: [], 1: []}
+        for unit in units:
+            dx, dy, k = unit // 8, unit // 4 % 2, unit % 4
+            sx, sy, sz = source(dx, dy, k)
+            left, right = [], []
+            for score in range(2):
+                spot = pl.multiple_of((score * 4 + sz) * SLAB, SLAB)
+                left.append(rows[0, sx, :, pl.ds(spot, SLAB)])
+                right.append(pl.ds(pl.multiple_of(sx * HALF + spot, SLAB), SLAB))
+            terms[dy].append((jnp.concatenate(left, axis=1), right))
+        for dy in range(2):
+            if not terms[dy]:
+                continue
+            half = (1 - y) if dy else y
+            left = jnp.concatenate([term[0] for term in terms[dy]], axis=1)
+            for start in range(0, HALF, 256):
+                right = [reach[half, spot, start:start + 256] for term in terms[dy] for spot in term[1]]
+                product = jnp.dot(left, jnp.concatenate(right, axis=0), preferred_element_type=jnp.float32)
+                if fresh:
+                    total[half, :, start:start + 256] = product
+                else:
+                    total[half, :, start:start + 256] += product
+
+    def columns(sz, score):
+        return pl.ds(pl.multiple_of((score * 4 + sz) * SLAB, SLAB), SLAB)
+
+    def partial(places, start, source):
+        left, right = [], []
+        for k in places:
+            _, _, sz = source(0, 0, k)
+            for score in range(2):
+                spot = columns(sz, score)
+                left.append(rows[1, y, :, spot])
+                first = pl.multiple_of(y * HALF + (score * 4 + sz) * SLAB, SLAB)
+                right.append(reach[1 - y, pl.ds(first, SLAB), start:start + 256])
+        return jnp.dot(
+            jnp.concatenate(left, axis=1), jnp.concatenate(right, axis=0), preferred_element_type=jnp.float32
+        )
+
+    counts = []
+
     def gather(end_case):
         places = (0, 1, 2, 3) if end_case else (1, 0, 2, 3)
 
@@ -123,48 +171,6 @@
                 sent[p] += 1
                 copy(p, sx, sy, sz, core, peers[hop], send_sem.at[p], recv_sem.at[p, sx, sy, sz]).start()
             copy(p, sx, sy, sz, core, mate, pass_sem.at[p], got_sem.at[p, sx, sy, sz]).start()
-
-        def first_product(units, fresh):
-            terms = {0: [], 1: []}
-            for unit in units:
-                dx, dy, k = unit // 8, unit // 4 % 2, unit % 4
-                sx, sy, sz = source(dx, dy, k)
-                for p in range(len(PIECES)):
-                    copy(p, sx, sy, sz, 1 - core, mate, pass_sem.at[p], got_sem.at[p, sx, sy, sz]).wait_recv()
-                left, right = [], []
-                for score in range(2):
-                    spot = pl.multiple_of((score * 4 + sz) * SLAB, SLAB)
-                    left.append(rows[0, sx, :, pl.ds(spot, SLAB)])
-                    right.append(pl.ds(pl.multiple_of(sx * HALF + spot, SLAB), SLAB))
-                terms[dy].append((jnp.concatenate(left, axis=1), right))
-            for dy in range(2):
-                if not terms[dy]:
-                    continue
-                half = (1 - y) if dy else y
-                left = jnp.concatenate([term[0] for term in terms[dy]], axis=1)
-                for start in range(0, HALF, 256):
-                    right = [reach[half, spot, start:start + 256] for term in terms[dy] for spot in term[1]]
-                    product = jnp.dot(left, jnp.concatenate(right, axis=0), preferred_element_type=jnp.float32)
-                    if fresh:
-                        total[half, :, start:start + 256] = product
-                    else:
-                        total[half, :, start:start + 256] += product
-
-        def columns(sz, score):
-            return pl.ds(pl.multiple_of((score * 4 + sz) * SLAB, SLAB), SLAB)
-
-        def partial(places, start):
-            left, right = [], []
-            for k in places:
-                _, _, sz = source(0, 0, k)
-                for score in range(2):
-                    spot = columns(sz, score)
-                    left.append(rows[1, y, :, spot])
-                    first = pl.multiple_of(y * HALF + (score * 4 + sz) * SLAB, SLAB)
-                    right.append(reach[1 - y, pl.ds(first, SLAB), start:start + 256])
-            return jnp.dot(
-                jnp.concatenate(left, axis=1), jnp.concatenate(right, axis=0), preferred_element_type=jnp.float32
-            )
 
         def second_product():
             for start in range(0, HALF, 256):
@@ -186,7 +192,7 @@
             @pl.when(x != y)
             def _():
                 for start in range(0, HALF, 256):
-                    more[1 - y, :, start:start + 256] = partial((0,), start)
+                    more[1 - y, :, start:start + 256] = partial((0,), start, source)
 
         def first_push(inwards):
             for p in range(len(PIECES)):
@@ -216,27 +222,13 @@
             if place in groups:
                 if fresh:
                     rows[0, 1 - y] = reach[1 - y, pl.ds(own_row, SLAB), :]
-                first_product(groups[place], fresh)
+                await_mate(groups[place], source)
+                first_product(groups[place], fresh, source)
                 fresh = False
             if place == (END_SECOND if end_case else MID_SECOND):
                 second_product()
 
-        first_product(LAST_GROUP, False)
-
-        @pl.when(x != y)
-        def _():
-            for start in range(0, HALF, 256):
-                more[1 - y, :, start:start + 256] += partial((1, 2, 3), start)
-
-        def drain(p, count, semaphore):
-            ref = reach.at[0, pl.ds(0, count * PIECES[p][2]), :]
-            pltpu.make_async_remote_copy(
-                src_ref=ref, dst_ref=ref, send_sem=semaphore, recv_sem=semaphore, device_id=mate, device_id_type=MESH
-            ).wait_send()
-
-        for p in range(len(PIECES)):
-            drain(p, sent[p], send_sem.at[p])
-            drain(p, 16, pass_sem.at[p])
+        counts.append(sent)
 
     @pl.when(end)
     def _():
@@ -246,6 +238,18 @@
     def _():
         gather(False)
 
+    def last_source(dx, dy, k):
+        place = k if k > 1 else jnp.where(end, 1, 0)
+        return (1 - x) if dx else x, (1 - y) if dy else y, jnp.where(upper, 3 - place, place)
+
+    await_mate(LAST_GROUP, last_source)
+
+    @pl.when(x != y)
+    def _():
+        for start in range(0, HALF, 256):
+            more[1 - y, :, start:start + 256] += partial((1, 2, 3), start, last_source)
+
+    first_product(LAST_GROUP, False, last_source)
     for start in range(0, HALF, 256):
         grown = total[1 - y, :, start:start + 256] + rows[0, 1 - y, :, start:start + 256].astype(jnp.float32)
         rows[1, 1 - y, :, start:start + 256] = jnp.minimum(grown, 1.0).astype(jnp.bfloat16)
@@ -274,6 +278,25 @@
 
     for start in range(0, HALF, 1024):
         out_ref[:, start:start + 1024] = block(0, y, start, 1024)
+
+    def drain(p, count, semaphore):
+        ref = reach.at[0, pl.ds(0, count * PIECES[p][2]), :]
+        pltpu.make_async_remote_copy(
+            src_ref=ref, dst_ref=ref, send_sem=semaphore, recv_sem=semaphore, device_id=mate, device_id_type=MESH
+        ).wait_send()
+
+    def drain_all(sent):
+        for p in range(len(PIECES)):
+            drain(p, sent[p], send_sem.at[p])
+            drain(p, 16, pass_sem.at[p])
+
+    @pl.when(end)
+    def _():
+        drain_all(counts[0])
+
+    @pl.when(jnp.logical_not(end))
+    def _():
+        drain_all(counts[1])
 
 
 def solution(mesh):

time: 52.1 us -> 52 us (level)
  no operation moved by 1% of the time
where the time goes in v14:
time: 52 us; the launch traced here: 51.4 us
  Pallas kernels  50.7 us (98%)
  local copies, waits for them, and re-layouts  0.71 us (1%)
    pallas_call x1, Pallas kernels, local(): pl.pallas_call(kernel, out_shape=pltpu.VMEM((SLAB, HALF), jnp.bfloat16),...  50.7 us

profile of v14, /device:TPU:0, one launch (start us, length us, event | category | flops | bytes accessed | tf_op | source)
XLA Modules:
  0.0 51.4 jit_solution(991508075974179129)
XLA Ops:
  0.0 50.7 %shard_map.17 = bf16[128,1024]{1,0:T(8,128)(2,1)S(1)} custom-call(bf16[128,1024]{1,0:T(8,128)(2,1)} %in_ref.1), custom_call_target="tpu_custom_call" | custom-call | tf_op jit(solution)/shard_map/pallas_call | solution.py:307
  50.7 0.7 %copy.3 = bf16[128,1024]{1,0:T(8,128)(2,1)} copy(bf16[128,1024]{1,0:T(8,128)(2,1)S(1)} %shard_map.17) | data formatting | bytes 524288

commit v15 on v14

--- a/solution.py
+++ b/solution.py
@@ -23,7 +23,6 @@
 
 END_GROUPS = ((10, (0, 1, 8, 4)), (24, (2, 9, 5, 12)), (36, (3, 10, 6)), (41, (11, 7)), (43, (13,)))
 MID_GROUPS = ((13, (0, 1, 8, 2, 4)), (29, (3, 9)), (34, (10, 5, 6, 12)), (43, (11, 7, 13)))
-LAST_GROUP = (14, 15)
 END_SECOND = 41
 MID_SECOND = 43
 
@@ -104,16 +103,19 @@
             src_ref=ref, dst_ref=ref, send_sem=send, recv_sem=recv, device_id=peer, device_id_type=MESH
         )
 
+    def parts(unit):
+        return unit if isinstance(unit, tuple) else (unit // 8, unit // 4 % 2, unit % 4)
+
     def await_mate(units, source):
         for unit in units:
-            sx, sy, sz = source(unit // 8, unit // 4 % 2, unit % 4)
+            sx, sy, sz = source(*parts(unit))
             for p in range(len(PIECES)):
                 copy(p, sx, sy, sz, 1 - core, mate, pass_sem.at[p], got_sem.at[p, sx, sy, sz]).wait_recv()
 
     def first_product(units, fresh, source):
         terms = {0: [], 1: []}
         for unit in units:
-            dx, dy, k = unit // 8, unit // 4 % 2, unit % 4
+            dx, dy, k = parts(unit)
             sx, sy, sz = source(dx, dy, k)
             left, right = [], []
             for score in range(2):
@@ -239,17 +241,22 @@
         gather(False)
 
     def last_source(dx, dy, k):
-        place = k if k > 1 else jnp.where(end, 1, 0)
+        place = jnp.where(end, 1, 0) if isinstance(k, int) else k
         return (1 - x) if dx else x, (1 - y) if dy else y, jnp.where(upper, 3 - place, place)
 
-    await_mate(LAST_GROUP, last_source)
-
-    @pl.when(x != y)
-    def _():
-        for start in range(0, HALF, 256):
-            more[1 - y, :, start:start + 256] += partial((1, 2, 3), start, last_source)
-
-    first_product(LAST_GROUP, False, last_source)
+    def more_of(places):
+        @pl.when(x != y)
+        def _():
+            for start in range(0, HALF, 256):
+                more[1 - y, :, start:start + 256] += partial(places, start, last_source)
+
+    early, late = jnp.where(end, 3, 2), jnp.where(end, 2, 3)
+    await_mate([(1, 1, early)], last_source)
+    first_product([(1, 1, early)], False, last_source)
+    more_of((1, early))
+    await_mate([(1, 1, late)], last_source)
+    more_of((late,))
+    first_product([(1, 1, late)], False, last_source)
     for start in range(0, HALF, 256):
         grown = total[1 - y, :, start:start + 256] + rows[0, 1 - y, :, start:start + 256].astype(jnp.float32)
         rows[1, 1 - y, :, start:start + 256] = jnp.minimum(grown, 1.0).astype(jnp.bfloat16)

time: 52 us -> 51.9 us (level)
  no operation moved by 1% of the time
where the time goes in v15:
time: 51.9 us; the launch traced here: 51.4 us
  Pallas kernels  50.7 us (98%)
  local copies, waits for them, and re-layouts  0.71 us (1%)
    pallas_call x1, Pallas kernels, local(): pl.pallas_call(kernel, out_shape=pltpu.VMEM((SLAB, HALF), jnp.bfloat16),...  50.7 us

profile of v15, /device:TPU:0, one launch (start us, length us, event | category | flops | bytes accessed | tf_op | source)
XLA Modules:
  0.0 51.4 jit_solution(8416117366449815233)
XLA Ops:
  0.0 50.7 %shard_map.17 = bf16[128,1024]{1,0:T(8,128)(2,1)S(1)} custom-call(bf16[128,1024]{1,0:T(8,128)(2,1)} %in_ref.1), custom_call_target="tpu_custom_call" | custom-call | tf_op jit(solution)/shard_map/pallas_call | solution.py:314
  50.7 0.7 %copy.3 = bf16[128,1024]{1,0:T(8,128)(2,1)} copy(bf16[128,1024]{1,0:T(8,128)(2,1)S(1)} %shard_map.17) | data formatting | bytes 524288

commit v16 on v15

--- a/solution.py
+++ b/solution.py
@@ -21,7 +21,7 @@
     43, 45, 44, 7, 11, 47, 13, 14, 27, 46, 23, 29, 30, 15, 31,
 )
 
-END_GROUPS = ((10, (0, 1, 8, 4)), (24, (2, 9, 5, 12)), (36, (3, 10, 6)), (41, (11, 7)), (43, (13,)))
+END_GROUPS = ((10, (0, 1, 8, 4)), (24, (2, 9, 5, 12)), (36, (3, 10, 6)), (41, (11, 7)), (44, (13,)))
 MID_GROUPS = ((13, (0, 1, 8, 2, 4)), (29, (3, 9)), (34, (10, 5, 6, 12)), (43, (11, 7, 13)))
 END_SECOND = 41
 MID_SECOND = 43
@@ -152,6 +152,7 @@
             jnp.concatenate(left, axis=1), jnp.concatenate(right, axis=0), preferred_element_type=jnp.float32
         )
 
+    flipped = (x == 0) & (y == 1)
     counts = []
 
     def gather(end_case):
@@ -214,13 +215,27 @@
 
         first_push(False)
         rows[0, y] = reach[y, pl.ds(own_row, SLAB), :]
-        groups = dict(END_GROUPS if end_case else MID_GROUPS)
-        fresh = True
-        for place, code in enumerate(END_ORDER if end_case else MID_ORDER):
+        def take(code):
             p, dx, dy, k = code // 16, code // 8 % 2, code // 4 % 2, code % 4
             sx, sy, sz = source(dx, dy, k)
             copy(p, sx, sy, sz, core, mate, send_sem.at[p], recv_sem.at[p, sx, sy, sz]).wait_recv()
             push(p, dx, dy, k)
+
+        groups = dict(END_GROUPS if end_case else MID_GROUPS)
+        fresh = True
+        for place, code in enumerate(END_ORDER if end_case else MID_ORDER):
+            if end_case and place == 43:
+                @pl.when(flipped)
+                def _():
+                    take(END_ORDER[44])
+                    take(END_ORDER[43])
+
+                @pl.when(jnp.logical_not(flipped))
+                def _():
+                    take(END_ORDER[43])
+                    take(END_ORDER[44])
+            elif not (end_case and place == 44):
+                take(code)
             if place in groups:
                 if fresh:
                     rows[0, 1 - y] = reach[1 - y, pl.ds(own_row, SLAB), :]
@@ -250,7 +265,8 @@
             for start in range(0, HALF, 256):
                 more[1 - y, :, start:start + 256] += partial(places, start, last_source)
 
-    early, late = jnp.where(end, 3, 2), jnp.where(end, 2, 3)
+    last_is_second = end & jnp.logical_not(flipped)
+    early, late = jnp.where(last_is_second, 3, 2), jnp.where(last_is_second, 2, 3)
     await_mate([(1, 1, early)], last_source)
     first_product([(1, 1, early)], False, last_source)
     more_of((1, early))

time: 51.9 us -> 51.7 us (level)
  no operation moved by 1% of the time
where the time goes in v16:
time: 51.7 us; the launch traced here: 51.4 us
  Pallas kernels  50.7 us (98%)
  local copies, waits for them, and re-layouts  0.71 us (1%)
    pallas_call x1, Pallas kernels, local(): pl.pallas_call(kernel, out_shape=pltpu.VMEM((SLAB, HALF), jnp.bfloat16),...  50.7 us

profile of v16, /device:TPU:0, one launch (start us, length us, event | category | flops | bytes accessed | tf_op | source)
XLA Modules:
  0.0 51.4 jit_solution(1938978504335910775)
XLA Ops:
  0.0 50.7 %shard_map.17 = bf16[128,1024]{1,0:T(8,128)(2,1)S(1)} custom-call(bf16[128,1024]{1,0:T(8,128)(2,1)} %in_ref.1), custom_call_target="tpu_custom_call" | custom-call | tf_op jit(solution)/shard_map/pallas_call | solution.py:330
  50.7 0.7 %copy.3 = bf16[128,1024]{1,0:T(8,128)(2,1)} copy(bf16[128,1024]{1,0:T(8,128)(2,1)S(1)} %shard_map.17) | data formatting | bytes 524288

commit v17 on v16

--- a/solution.py
+++ b/solution.py
@@ -294,7 +294,8 @@
 
     def step(now):
         for half in range(2):
-            rows[1 - now, half] = block(now, half, 0, HALF)
+            for start in range(0, HALF, 512):
+                rows[1 - now, half, :, start:start + 512] = block(now, half, start, 512)
 
     for count in range(STEPS - 3):
         step(count % 2)

time: 51.7 us -> 51.7 us (level)
  no operation moved by 1% of the time
where the time goes in v17:
time: 51.7 us; the launch traced here: 51.5 us
  Pallas kernels  50.7 us (98%)
  local copies, waits for them, and re-layouts  0.71 us (1%)
    pallas_call x1, Pallas kernels, local(): pl.pallas_call(kernel, out_shape=pltpu.VMEM((SLAB, HALF), jnp.bfloat16),...  50.7 us

profile of v17, /device:TPU:0, one launch (start us, length us, event | category | flops | bytes accessed | tf_op | source)
XLA Modules:
  0.0 51.5 jit_solution(1773756235669807557)
XLA Ops:
  0.0 50.7 %shard_map.17 = bf16[128,1024]{1,0:T(8,128)(2,1)S(1)} custom-call(bf16[128,1024]{1,0:T(8,128)(2,1)} %in_ref.1), custom_call_target="tpu_custom_call" | custom-call | tf_op jit(solution)/shard_map/pallas_call | solution.py:331
  50.8 0.7 %copy.3 = bf16[128,1024]{1,0:T(8,128)(2,1)} copy(bf16[128,1024]{1,0:T(8,128)(2,1)S(1)} %shard_map.17) | data formatting | bytes 524288

commit v18 on v16

--- a/solution.py
+++ b/solution.py
@@ -21,8 +21,8 @@
     43, 45, 44, 7, 11, 47, 13, 14, 27, 46, 23, 29, 30, 15, 31,
 )
 
-END_GROUPS = ((10, (0, 1, 8, 4)), (24, (2, 9, 5, 12)), (36, (3, 10, 6)), (41, (11, 7)), (44, (13,)))
-MID_GROUPS = ((13, (0, 1, 8, 2, 4)), (29, (3, 9)), (34, (10, 5, 6, 12)), (43, (11, 7, 13)))
+END_GROUPS = ((14, (0, 1, 8, 4)), (24, (2, 9, 5, 12)), (36, (3, 10, 6)), (41, (11, 7)), (44, (13,)))
+MID_GROUPS = ((17, (0, 1, 8, 2, 4)), (29, (3, 9)), (34, (10, 5, 6, 12)), (43, (11, 7, 13)))
 END_SECOND = 41
 MID_SECOND = 43
 

time: 51.7 us -> 51.7 us (level)
  no operation moved by 1% of the time
where the time goes in v18:
time: 51.7 us; the launch traced here: 51.4 us
  Pallas kernels  50.7 us (98%)
  local copies, waits for them, and re-layouts  0.71 us (1%)
    pallas_call x1, Pallas kernels, local(): pl.pallas_call(kernel, out_shape=pltpu.VMEM((SLAB, HALF), jnp.bfloat16),...  50.7 us

profile of v18, /device:TPU:0, one launch (start us, length us, event | category | flops | bytes accessed | tf_op | source)
XLA Modules:
  0.0 51.4 jit_solution(273836971741017671)
XLA Ops:
  0.0 50.7 %shard_map.17 = bf16[128,1024]{1,0:T(8,128)(2,1)S(1)} custom-call(bf16[128,1024]{1,0:T(8,128)(2,1)} %in_ref.1), custom_call_target="tpu_custom_call" | custom-call | tf_op jit(solution)/shard_map/pallas_call | solution.py:330
  50.7 0.7 %copy.3 = bf16[128,1024]{1,0:T(8,128)(2,1)} copy(bf16[128,1024]{1,0:T(8,128)(2,1)S(1)} %shard_map.17) | data formatting | bytes 524288
